TPU v7x, 32 devices: a whole 2x2x4 slice. The times are simulated.
32 devices in a mesh: groups: 2 (over x), cols: 4 (over y, core), rows: 4 (over z).
Axes of the slice: x: 2, y: 2, z: 4, core: 2. Of those that a mesh axis runs over, the one named last changes fastest.
Arguments:
- camera_tokens: bfloat16 [1024, 6144], P(('groups', 'rows'), 'cols'), parts along dimension 0, may hold values from -150 to 150, as said below
- norm_gain: float32 [6144], P('cols'), may hold values from 0.25 to 1.75
- query_weight: bfloat16 [6144, 6144], P('cols', 'rows'), may hold values from -0.078125 to 0.078125
- key_weight: bfloat16 [6144, 6144], P('cols', 'rows'), may hold values from -0.078125 to 0.078125
- value_weight: bfloat16 [6144, 6144], P('cols', 'rows'), may hold values from -0.078125 to 0.078125
- query_gain: float32 [6144], P('rows'), may hold values from 0.5 to 14, as said below
- key_gain: float32 [6144], P('rows'), may hold values from 0.5 to 14, as said below
- out_weight: bfloat16 [6144, 6144], P('rows', 'cols'), may hold values from -0.078125 to 0.078125
- up_weight: bfloat16 [6144, 24576], P('cols', 'rows'), may hold values from -0.078125 to 0.078125
- up_bias: float32 [24576], P('rows'), may hold values from -3 to 3
- down_weight: bfloat16 [24576, 6144], P('rows', 'cols'), may hold values from -0.0390625 to 0.0390625
- down_bias: float32 [6144], P('cols'), may hold values from -3 to 3
- join_gain: float32 [6144], P('cols'), may hold values from 0.25 to 1.75
- join_query: bfloat16 [6144, 6144], P('cols', 'rows'), may hold values from -0.078125 to 0.078125
- join_key: bfloat16 [6144, 6144], P('cols', 'rows'), may hold values from -0.078125 to 0.078125
- join_value: bfloat16 [6144, 6144], P('cols', 'rows'), may hold values from -0.078125 to 0.078125
- join_query_gain: float32 [6144], P('rows'), may hold values from 0.5 to 14, as said below
- join_key_gain: float32 [6144], P('rows'), may hold values from 0.5 to 14, as said below
- join_out: bfloat16 [6144, 6144], P('rows', 'cols'), may hold values from -0.078125 to 0.078125
Outputs:
- joined_tokens: bfloat16 [1024, 6144], P(('groups', 'rows'), 'cols'), parts along dimension 0
There are 2 independent parts, one for each index of `groups`. A program takes and returns all parts, laid end to end along the dimension named above; an argument that names none is the same for every part. Nothing has to cross between parts.
Inputs may be any that keep to these rules, and one draw needn't show every extreme that they name: `camera_tokens`: real valued tokens. `query_gain`: Positive. `key_gain`: Positive. `join_query_gain`: Positive. `join_key_gain`: Positive.
All inputs are finite; a program needn't handle non-finite values.
Results may differ from a plain program's by a relative error of at most 0.012.
Values may be sent and summed in bfloat16 or wider, within the bound.
A program may use at most 192 MiB of HBM per device.

v0:
```python
import functools
import math

import jax
import jax.numpy as jnp
from jax import lax
from jax.experimental import pallas as pl
from jax.experimental.pallas import tpu as pltpu
from jax.sharding import PartitionSpec as P

HEAD_DIM = 128
TOK_CAM = 64
D = 6144


EPS = 1e-06


def partner_2(array, axis, bit):
    return lax.ppermute(array, axis, [(i, i ^ 1 << bit) for i in range(lax.axis_size(axis))])


def normalize(values, scales, moments):
    row_mean = moments[0] / D
    row_var = moments[1] / D - row_mean * row_mean
    return ((values - row_mean[:, None]) * lax.rsqrt(row_var[:, None] + EPS) * scales).astype(
        jnp.bfloat16
    )


def shard_moments(values):
    return lax.psum((jnp.sum(values, 1), jnp.sum(values * values, 1)), "cols")


def head_norm(values, scales):
    row_count = values.shape[0]
    grouped = values.reshape(row_count, -1, HEAD_DIM)
    row_mean = jnp.mean(grouped, -1, keepdims=True)
    row_var = jnp.mean(grouped * grouped, -1, keepdims=True) - row_mean * row_mean
    normed = (grouped - row_mean) * lax.rsqrt(row_var + EPS)
    return (normed.reshape(row_count, -1) * scales).astype(jnp.bfloat16)


def attend(queries, key_rows, val_rows):
    inv_root = 1.0 / math.sqrt(HEAD_DIM)
    scores = (
        jnp.einsum("bqhd,bkhd->bhqk", queries, key_rows, preferred_element_type=jnp.float32)
        * inv_root
    )
    row_max = jnp.max(scores, -1, keepdims=True)
    weights = jnp.exp(scores - row_max)
    row_sum = jnp.sum(weights, -1)
    blended = jnp.einsum(
        "bhqk,bkhd->bqhd",
        weights.astype(jnp.bfloat16),
        val_rows,
        preferred_element_type=jnp.float32,
    )
    return blended / jnp.transpose(row_sum, (0, 2, 1))[..., None]


def to_heads(matrix, blocks):
    return matrix.reshape(blocks, -1, matrix.shape[1] // HEAD_DIM, HEAD_DIM)


def camera_attention(queries, key_rows, val_rows):
    local_rows = queries.shape[0]
    if local_rows >= TOK_CAM:
        blocks = local_rows // TOK_CAM
        result = attend(
            to_heads(queries, blocks), to_heads(key_rows, blocks), to_heads(val_rows, blocks)
        )
    else:
        cam_span = TOK_CAM // local_rows
        position = lax.axis_index("cols")
        key_value = jnp.stack((key_rows, val_rows))
        for which_bit in range(cam_span.bit_length() - 1):
            partner = partner_2(key_value, "cols", which_bit)
            is_lower = position >> which_bit & 1 == 0
            key_value = jnp.where(
                is_lower,
                jnp.concatenate((key_value, partner), 1),
                jnp.concatenate((partner, key_value), 1),
            )
        result = attend(to_heads(queries, 1), to_heads(key_value[0], 1), to_heads(key_value[1], 1))
    return result.reshape(local_rows, -1).astype(jnp.bfloat16)


def plain_body(
    camera_tokens,
    norm_gain,
    query_weight,
    key_weight,
    value_weight,
    query_gain,
    key_gain,
    out_weight,
    up_weight,
    up_bias,
    down_weight,
    down_bias,
    join_gain,
    join_query,
    join_key,
    join_value,
    join_query_gain,
    join_key_gain,
    join_out,
):
    own_rows = camera_tokens.shape[0]
    all_rows = own_rows * lax.axis_size("rows")
    col_rows = all_rows // lax.axis_size("cols")
    attn_width = query_weight.shape[1]
    start_f32 = camera_tokens.astype(jnp.float32)
    normed_all = lax.all_gather(
        normalize(start_f32, norm_gain, shard_moments(start_f32)), "rows", axis=0, tiled=True
    )
    joint_weight = jnp.concatenate((query_weight, key_weight, value_weight, up_weight), 1)
    joint = lax.psum_scatter(
        jnp.dot(normed_all, joint_weight, preferred_element_type=jnp.float32),
        "cols",
        scatter_dimension=0,
        tiled=True,
    )
    up_sum = joint[:, 3 * attn_width :]
    hidden = jax.nn.gelu(up_sum + up_bias, approximate=False).astype(jnp.bfloat16)
    attended = camera_attention(
        head_norm(joint[:, :attn_width], query_gain),
        head_norm(joint[:, attn_width : 2 * attn_width], key_gain),
        joint[:, 2 * attn_width : 3 * attn_width].astype(jnp.bfloat16),
    )
    attn_all, hidden_all = (
        lax.all_gather(attended, "cols", axis=0, tiled=True),
        lax.all_gather(hidden, "cols", axis=0, tiled=True),
    )
    mixed = lax.psum_scatter(
        jnp.dot(attn_all, out_weight, preferred_element_type=jnp.float32)
        + jnp.dot(hidden_all, down_weight, preferred_element_type=jnp.float32),
        "rows",
        scatter_dimension=0,
        tiled=True,
    )
    layer_own = (start_f32 + mixed + down_bias).astype(jnp.bfloat16)
    layer_f32 = layer_own.astype(jnp.float32)
    join_in = lax.all_gather(
        normalize(layer_f32, join_gain, shard_moments(layer_f32)), "rows", axis=0, tiled=True
    )
    join_weight = jnp.concatenate((join_query, join_key, join_value), 1)
    join_joint = lax.psum_scatter(
        jnp.dot(join_in, join_weight, preferred_element_type=jnp.float32),
        "cols",
        scatter_dimension=0,
        tiled=True,
    )
    join_q = head_norm(join_joint[:, :attn_width], join_query_gain)
    join_k = head_norm(join_joint[:, attn_width : 2 * attn_width], join_key_gain)
    join_v = join_joint[:, 2 * attn_width :].astype(jnp.bfloat16)
    heads_here = attn_width // HEAD_DIM
    query_heads = join_q.reshape(col_rows, heads_here, HEAD_DIM)
    inv_root = 1.0 / math.sqrt(HEAD_DIM)
    run_max = jnp.full((heads_here, col_rows), -jnp.inf, jnp.float32)
    run_sum = jnp.zeros((heads_here, col_rows), jnp.float32)
    accum = jnp.zeros((col_rows, heads_here, HEAD_DIM), jnp.float32)
    key_part = lax.all_gather(join_k, "cols", axis=0, tiled=True)
    val_part = lax.all_gather(join_v, "cols", axis=0, tiled=True)
    row_count = key_part.shape[0]
    key_heads = key_part.reshape(row_count, heads_here, HEAD_DIM)
    val_heads = val_part.reshape(row_count, heads_here, HEAD_DIM)
    scores = (
        jnp.einsum("qhd,khd->hqk", query_heads, key_heads, preferred_element_type=jnp.float32)
        * inv_root
    )
    new_max = jnp.max(scores, -1)
    factor = jnp.exp(run_max - new_max)
    weights = jnp.exp(scores - new_max[..., None])
    run_sum = run_sum * factor + jnp.sum(weights, -1)
    accum = accum * jnp.transpose(factor)[..., None] + jnp.einsum(
        "hqk,khd->qhd", weights.astype(jnp.bfloat16), val_heads, preferred_element_type=jnp.float32
    )
    run_max, run_sum, accum = (new_max, run_sum, accum)
    joined_attn = (
        (accum / jnp.transpose(run_sum)[..., None])
        .reshape(col_rows, attn_width)
        .astype(jnp.bfloat16)
    )
    joined_all = lax.all_gather(joined_attn, "cols", axis=0, tiled=True)
    result = lax.psum_scatter(
        jnp.dot(joined_all, join_out, preferred_element_type=jnp.float32),
        "rows",
        scatter_dimension=0,
        tiled=True,
    )
    return (layer_own.astype(jnp.float32) + result).astype(jnp.bfloat16)


F32 = jnp.float32
BF16 = jnp.bfloat16
MESH = pl.DeviceIdType.MESH
VMEM_LIMIT = 66 * 1024 * 1024 - 3 * 1024 * 1024


def each(count, step):
    lax.fori_loop(0, count, lambda i, carry: (step(i), carry)[1], None)


def remote(src, dst, send, recv, device):
    return pltpu.make_async_remote_copy(
        src_ref=src,
        dst_ref=dst,
        send_sem=send,
        recv_sem=recv,
        device_id=device,
        device_id_type=MESH,
    )


def places():
    col = lax.axis_index("cols")
    core = lax.rem(col, 2)
    return col, col + 1 - 2 * core, lax.rem(col + 2, 4)


def greet(cols_away):
    col, row, row_count = lax.axis_index("cols"), lax.axis_index("rows"), lax.axis_size("rows")
    barrier = pltpu.get_barrier_semaphore()
    _, mate, across = places()
    others = {1: mate, 2: across}
    if cols_away == 3:
        others[3] = mate + across - col
    for other in others.values():
        pl.semaphore_signal(barrier, inc=1, device_id={"cols": other}, device_id_type=MESH)

    @pl.when(row > 0)
    def _():
        pl.semaphore_signal(barrier, inc=1, device_id={"rows": row - 1}, device_id_type=MESH)

    @pl.when(row < row_count - 1)
    def _():
        pl.semaphore_signal(barrier, inc=1, device_id={"rows": row + 1}, device_id_type=MESH)

    inner = (row > 0) & (row < row_count - 1)

    @pl.when(inner)
    def _():
        pl.semaphore_wait(barrier, len(others) + 2)

    @pl.when(jnp.logical_not(inner))
    def _():
        pl.semaphore_wait(barrier, len(others) + 1)


def gather_rows(normed, send_r, send_l, arrive):
    row, row_count = lax.axis_index("rows"), lax.axis_size("rows")

    def to_right(block):
        return remote(
            normed.at[block], normed.at[block], send_r.at[block], arrive.at[block], {"rows": row + 1}
        )

    def to_left(block):
        return remote(
            normed.at[block], normed.at[block], send_l.at[block], arrive.at[block], {"rows": row - 1}
        )

    def pass_on(from_left, block):
        if from_left:

            @pl.when(row < row_count - 1)
            def _():
                to_right(block).start()
        else:

            @pl.when(row > 0)
            def _():
                to_left(block).start()

    pass_on(True, row)
    pass_on(False, row)

    def take(away):
        @pl.when(row >= away)
        def _():
            to_right(row - away).wait_recv()
            pass_on(True, row - away)

        @pl.when(row + away < row_count)
        def _():
            to_left(row + away).wait_recv()
            pass_on(False, row + away)

    def finish():
        for block in range(row_count):

            @pl.when((row >= block) & (row < row_count - 1))
            def _():
                to_right(block).wait_send()

            @pl.when((row <= block) & (row > 0))
            def _():
                to_left(block).wait_send()

    return take, finish


def norm_heads(values, scales):
    parts = []
    for start in range(0, values.shape[1], HEAD_DIM):
        part = values[:, start : start + HEAD_DIM]
        mean = jnp.mean(part, -1, keepdims=True)
        var = jnp.mean(part * part, -1, keepdims=True) - mean * mean
        parts.append((part - mean) * lax.rsqrt(var + EPS))
    return (jnp.concatenate(parts, 1) * scales).astype(BF16)


def soft_blend(query, keys, values):
    scores = lax.dot_general(
        query, keys, (((1,), (1,)), ((), ())), preferred_element_type=F32
    ) * (1.0 / math.sqrt(HEAD_DIM))
    weights = jnp.exp(scores - jnp.max(scores, -1, keepdims=True))
    total = jnp.sum(weights, -1, keepdims=True)
    blended = jnp.dot(weights.astype(BF16), values, preferred_element_type=F32)
    return (blended / total).astype(BF16)


def in_kernel(span, has_up, width, *refs, follow=None):
    refs = list(refs)
    tokens, gain, q_gain, k_gain, wq, wk, wv = refs[:7]
    refs = refs[7:]
    if has_up:
        bias, w_up = refs[:2]
        refs = refs[2:]
    out_a = refs.pop(0)
    if has_up:
        out_u = refs.pop(0)
    normed, moments, m_send, m_recv, z_right, z_left, z_arrive, queries, keys, values = refs[:10]
    groups = [refs[10:25]]
    if has_up:
        groups.append(refs[25:40])
    col, mate, across = places()
    diagonal = mate + across - col
    row, row_count = lax.axis_index("rows"), lax.axis_size("rows")
    own_rows = tokens.shape[0]
    near = row_count // 2

    def load(group, unit, owner, source, start):
        held = group[0]
        columns = pl.ds(pl.multiple_of(start, HEAD_DIM), held.shape[-1])
        return pltpu.make_async_copy(
            source.at[:, columns], held.at[unit * 4 + owner], group[6].at[unit * 4 + owner]
        )

    def loads(group_id, unit, owner, which=None):
        group = groups[group_id]
        wide = group[0].shape[-1]
        if group_id == 0:
            return load(group, unit, owner, (wq, wk, wv)[which], owner * wide)
        return load(group, unit, owner, w_up, owner * (groups[1][5].shape[0] * wide) + unit * wide)

    def start_loads(owner):
        for which in range(3):
            loads(0, which, owner, which).start()
        if has_up:
            each(groups[1][5].shape[0], lambda unit: loads(1, unit, owner).start())

    order = (diagonal, across, mate, col)
    for owner in order:
        start_loads(owner)
    greet(3)

    own = tokens[...].astype(F32)
    lane = lax.broadcasted_iota(jnp.int32, (own_rows, HEAD_DIM), 1)
    mine = jnp.where(
        lane < HEAD_DIM // 2,
        jnp.sum(own, 1, keepdims=True),
        jnp.sum(own * own, 1, keepdims=True),
    )
    moments[3] = mine
    swaps = []
    for slot, other in enumerate((mate, across, diagonal)):
        swap = remote(
            moments.at[3], moments.at[slot], m_send.at[slot], m_recv.at[slot], {"cols": other}
        )
        swap.start()
        swaps.append(swap)
    for swap in swaps:
        swap.wait_recv()
    total = (moments[3] + moments[0]) + (moments[1] + moments[2])
    mean = total[:, :1] / width
    var = total[:, HEAD_DIM // 2 : HEAD_DIM // 2 + 1] / width - mean * mean
    normed[row] = ((own - mean) * lax.rsqrt(var + EPS) * gain[...].reshape(1, -1)).astype(BF16)
    take_rows, finish_rows = gather_rows(normed, z_right, z_left, z_arrive)
    for swap in swaps:
        swap.wait_send()

    def ops(group):
        held, f_send, f_recv, p_send, p_recv, own_sum, _, y_send, y_recv, fs, fr, ps, pr, ys, yr = group

        def product(unit, left, owner, fresh):
            weight = held.at[unit * 4 + owner]
            if fresh:
                pltpu.make_async_copy(weight, weight, group[6].at[unit * 4 + owner]).wait()
            return jnp.dot(left, weight[...], preferred_element_type=F32)

        def first_to_mate(unit, block):
            return remote(
                f_send.at[unit, block],
                f_recv.at[unit, block],
                fs.at[unit, block],
                fr.at[unit, block],
                {"cols": mate},
            )

        def second_to_mate(unit, half):
            return remote(
                p_send.at[unit, half],
                p_recv.at[unit, half],
                ps.at[unit, half],
                pr.at[unit, half],
                {"cols": mate},
            )

        def to_across(unit, block):
            return remote(
                y_send.at[unit, block],
                y_recv.at[unit, block],
                ys.at[unit, block],
                yr.at[unit, block],
                {"cols": across},
            )

        def first(block, fresh):
            def give(unit):
                f_send[unit, block] = product(unit, normed[block], diagonal, fresh).astype(BF16)
                first_to_mate(unit, block).start()

            def send(unit):
                partial = product(unit, normed[block], across, fresh)
                first_to_mate(unit, block).wait_recv()
                y_send[unit, block] = (partial + f_recv[unit, block].astype(F32)).astype(BF16)
                to_across(unit, block).start()

            each(own_sum.shape[0], give)
            each(own_sum.shape[0], send)

        def second(half, fresh):
            def rows_in():
                return normed[pl.ds(half * near, near)].reshape(near * own_rows, normed.shape[-1])

            def give(unit):
                p_send[unit, half] = product(unit, rows_in(), mate, fresh).astype(BF16)
                second_to_mate(unit, half).start()

            def keep(unit):
                partial = product(unit, rows_in(), col, fresh)
                second_to_mate(unit, half).wait_recv()
                own_sum[unit, half] = partial + p_recv[unit, half].astype(F32)

            each(own_sum.shape[0], give)
            each(own_sum.shape[0], keep)

        def final(unit, half):
            for place in range(near):
                to_across(unit, half * near + place).wait_recv()
            arrived = y_recv[unit, pl.ds(half * near, near)].astype(F32)
            return own_sum[unit, half] + arrived.reshape(near * own_rows, -1)

        def finish(unit):
            for block in range(row_count):
                first_to_mate(unit, block).wait_send()
                to_across(unit, block).wait_send()
            for half in range(2):
                second_to_mate(unit, half).wait_send()

        return first, second, final, finish, own_sum.shape[0]

    all_ops = [ops(group) for group in groups]
    home = row // near
    wide = groups[0][0].shape[-1]
    mine = pl.ds(pl.multiple_of(col * wide, HEAD_DIM), wide)
    half_rows = near * own_rows

    def firsts(block, fresh):
        for first, *_ in all_ops:
            first(block, fresh)

    def seconds(half, fresh):
        for _, second, *_ in all_ops:
            second(half, fresh)

    def camera(which):
        rows = pl.ds(pl.multiple_of(which * span, span), span)
        local = pl.ds(pl.multiple_of(lax.rem(which * span, half_rows), span), span)
        for start in range(0, wide, HEAD_DIM):
            head = slice(start, start + HEAD_DIM)
            out_a[which * span // half_rows, local, head] = soft_blend(
                queries[rows, head], keys[rows, head], values[rows, head]
            )

    def joint(half):
        for start in range(0, wide, HEAD_DIM):
            head = slice(start, start + HEAD_DIM)
            rows = pl.ds(pl.multiple_of(half * half_rows, half_rows), half_rows)
            blended = soft_blend(queries[rows, head], keys[:, head], values[:, head])
            out_a[0, pl.ds(half * near, near), :, head] = blended.reshape(near, own_rows, HEAD_DIM)

    def finals(half):
        final = all_ops[0][2]
        rows = pl.ds(pl.multiple_of(half * half_rows, half_rows), half_rows)
        queries[rows] = norm_heads(final(0, half), q_gain[mine].reshape(1, -1))
        keys[rows] = norm_heads(final(1, half), k_gain[mine].reshape(1, -1))
        values[rows] = final(2, half).astype(BF16)
        if span < half_rows:
            count = half_rows // span
            each(count, lambda which: camera(half * count + which))
        if has_up:
            up_final = all_ops[1][2]

            def activate(unit):
                raw = up_final(unit, half) + bias[col * out_u.shape[0] + unit]
                out_u[unit, half] = (raw * (1.0 + lax.erf(raw * math.sqrt(0.5))) * 0.5).astype(BF16)

            each(out_u.shape[0], activate)

    firsts(row, True)
    take_rows(1)
    firsts(row + 1 - 2 * lax.rem(row, 2), False)
    seconds(home, True)
    take_rows(2)
    firsts(near - home, False)
    take_rows(3)
    firsts((row_count - 1) * (1 - home), False)
    if has_up:
        finals(home)
        seconds(1 - home, False)
    else:
        seconds(1 - home, False)
        finals(home)
    finals(1 - home)
    if follow is not None:
        follow(joint)
    for first, second, final, finish, count in all_ops:
        each(count, finish)
    finish_rows()


def in_call(name, number, span, tokens, gain, q_gain, k_gain, weights, up=None, join=None):
    own_rows, depth = tokens.shape
    all_rows = own_rows * lax.axis_size("rows")
    cols = lax.axis_size("cols")
    wide = weights[0].shape[1] // cols
    groups = [(3, wide)]
    operands = [tokens, gain, q_gain, k_gain, *weights]
    any_spec, vmem_spec = pl.BlockSpec(memory_space=pl.ANY), pl.BlockSpec(memory_space=pltpu.VMEM)
    in_specs = [vmem_spec] * 4 + [any_spec] * 3
    half_rows = all_rows // 2
    out_shape = [jax.ShapeDtypeStruct((2, half_rows, wide), BF16)]
    if up is not None:
        up_bias, up_weight = up
        up_wide = up_tile(up_weight.shape[1] // cols)
        count = up_weight.shape[1] // cols // up_wide
        groups.append((count, up_wide))
        operands += [up_bias.reshape(cols * count, 1, up_wide), up_weight]
        in_specs += [vmem_spec, any_spec]
        out_shape.append(jax.ShapeDtypeStruct((count, 2, half_rows, up_wide), BF16))
    dma = pltpu.SemaphoreType.DMA
    row_count = lax.axis_size("rows")
    scratch = [
        pltpu.VMEM((row_count, own_rows, depth), BF16),
        pltpu.VMEM((4, own_rows, HEAD_DIM), F32),
        dma((3,)),
        dma((3,)),
        dma((row_count,)),
        dma((row_count,)),
        dma((row_count,)),
    ] + [pltpu.VMEM((all_rows, wide), BF16)] * 3
    for count, piece in groups:
        scratch += [
            pltpu.VMEM((count * 4, depth, piece), BF16),
            pltpu.VMEM((count, row_count, own_rows, piece), BF16),
            pltpu.VMEM((count, row_count, own_rows, piece), BF16),
            pltpu.VMEM((count, 2, half_rows, piece), BF16),
            pltpu.VMEM((count, 2, half_rows, piece), BF16),
            pltpu.VMEM((count, 2, half_rows, piece), F32),
            dma((count * 4,)),
            pltpu.VMEM((count, row_count, own_rows, piece), BF16),
            pltpu.VMEM((count, row_count, own_rows, piece), BF16),
            dma((count, row_count)),
            dma((count, row_count)),
            dma((count, 2)),
            dma((count, 2)),
            dma((count, row_count)),
            dma((count, row_count)),
        ]
    if join is not None:
        base_scratch = out_scratch([(1, wide)], own_rows, join.shape[1], row_count)
        return pl.pallas_call(
            functools.partial(join_kernel, span, float(depth * cols)),
            name=name,
            out_shape=jax.ShapeDtypeStruct((own_rows, join.shape[1]), BF16),
            in_specs=in_specs + [any_spec],
            out_specs=vmem_spec,
            scratch_shapes=[pltpu.VMEM((1, row_count, own_rows, wide), BF16)] + scratch + base_scratch,
            compiler_params=pltpu.CompilerParams(
                collective_id=number, has_side_effects=True, vmem_limit_bytes=VMEM_LIMIT
            ),
        )(*operands, join)
    return pl.pallas_call(
        functools.partial(in_kernel, span, up is not None, float(depth * cols)),
        name=name,
        out_shape=out_shape,
        in_specs=in_specs,
        out_specs=[vmem_spec] * len(out_shape),
        scratch_shapes=scratch,
        compiler_params=pltpu.CompilerParams(
            collective_id=number, has_side_effects=True, vmem_limit_bytes=VMEM_LIMIT
        ),
    )(*operands)


def out_kernel(has_up, *refs):
    for _ in out_steps(has_up, {}, *refs):
        pass


def join_kernel(span, width, tokens, gain, q_gain, k_gain, wq, wk, wv, w_out, result, heads, *rest):
    later = {}
    steps = out_steps(False, later, tokens, heads, w_out, result, *rest[25:])
    next(steps)

    def follow(joint):
        later["joint"] = joint
        for _ in steps:
            pass

    in_kernel(
        span, False, width, tokens, gain, q_gain, k_gain, wq, wk, wv, heads, *rest[:25], follow=follow
    )


def out_steps(has_up, later, *refs):
    refs = list(refs)
    base, heads, w_out = refs[:3]
    refs = refs[3:]
    if has_up:
        bias, hidden, w_down = refs[:3]
        refs = refs[3:]
    result, accum, right_send, left_send, from_left, from_right = refs[:6]
    r_send, r_recv, l_send, l_recv = refs[6:10]
    groups = [refs[10:18]]
    if has_up:
        groups.append(refs[18:26])
    col, mate, across = places()
    diagonal = mate + across - col
    row, row_count = lax.axis_index("rows"), lax.axis_size("rows")
    own_rows = base.shape[0]
    near = row_count // 2
    owners = (col, mate, across, diagonal)
    sources = [(heads, w_out)]
    if has_up:
        sources.append((hidden, w_down))

    def load(group_id, unit, place):
        held, sem = groups[group_id][0], groups[group_id][1]
        source = sources[group_id][1]
        deep = held.shape[1]
        count = held.shape[0] // 4
        start = pl.multiple_of((owners[place] * count + unit) * deep, HEAD_DIM)
        return pltpu.make_async_copy(
            source.at[pl.ds(start, deep)], held.at[place * count + unit], sem.at[place * count + unit]
        )

    for place in range(4):
        for group_id, group in enumerate(groups):
            each(group[0].shape[0] // 4, lambda unit: load(group_id, unit, place).start())
    yield
    joint = later.get("joint")
    if joint is None:
        greet(2)

    def part_of(ref, stage):
        return ref.at[pl.ds(stage[0], stage[1])]

    def read(ref, stage):
        return part_of(ref, stage)[...].reshape(stage[1] * own_rows, -1)

    def copies(group_id):
        _, _, got, y_send, p_send, f_send, y_recv, p_recv = groups[group_id]
        source = sources[group_id][0]

        def to_across(unit, half):
            return remote(
                part_of(source.at[unit], half),
                part_of(got.at[1, unit], half),
                y_send.at[unit, half[2]],
                y_recv.at[unit, half[2]],
                {"cols": across},
            )

        def to_mate(unit, half):
            return remote(
                part_of(source.at[unit], half),
                part_of(got.at[0, unit], half),
                p_send.at[unit, half[2]],
                p_recv.at[0, unit, half[2]],
                {"cols": mate},
            )

        def forward(unit, half):
            return remote(
                part_of(got.at[1, unit], half),
                part_of(got.at[2, unit], half),
                f_send.at[unit, half[2]],
                p_recv.at[1, unit, half[2]],
                {"cols": mate},
            )

        return to_across, to_mate, forward, groups[group_id][0].shape[0] // 4

    moves = [copies(group_id) for group_id in range(len(groups))]
    home = row // near
    pair = row + 1 - 2 * lax.rem(row, 2)
    stages = (((1 - home) * near, near, 0), (pair, 1, 1), (row, 1, 2))

    def share(half):
        for to_across, to_mate, forward, count in moves:
            each(count, lambda unit: to_across(unit, half).start())
            each(count, lambda unit: to_mate(unit, half).start())

    if joint is not None:
        joint(1 - home)
    share(stages[0])
    if joint is None:
        share(stages[1])
        share(stages[2])

    def add(group_id, unit, place, half, fresh, piece, begin=False):
        if fresh:
            load(group_id, unit, place).wait()
        held = groups[group_id][0]
        count = held.shape[0] // 4
        part = jnp.dot(piece, held[place * count + unit], preferred_element_type=F32)
        part = part.reshape(half[1], own_rows, -1)
        if begin:
            part_of(accum, half)[...] = part
        else:
            part_of(accum, half)[...] += part

    def near_chunks(half, fresh):
        for group_id, (to_across, to_mate, forward, count) in enumerate(moves):
            source, got = sources[group_id][0], groups[group_id][2]
            if group_id == 0:
                add(0, 0, 0, half, fresh, read(source.at[0], half), True)
            else:
                each(count, lambda unit: add(group_id, unit, 0, half, fresh, read(source.at[unit], half)))

            def from_mate(unit):
                to_mate(unit, half).wait_recv()
                add(group_id, unit, 1, half, fresh, read(got.at[0, unit], half))

            each(count, from_mate)

    def far_chunks(half, fresh):
        for group_id, (to_across, to_mate, forward, count) in enumerate(moves):
            got = groups[group_id][2]

            def from_across(unit):
                to_across(unit, half).wait_recv()
                forward(unit, half).start()
                add(group_id, unit, 2, half, fresh, read(got.at[1, unit], half))
                forward(unit, half).wait_recv()
                add(group_id, unit, 3, half, fresh, read(got.at[2, unit], half))

            each(count, from_across)

    piece_wide = from_left.shape[-1]
    pieces = from_left.shape[1]

    def term(block, piece):
        return accum[block, :, piece * piece_wide : (piece + 1) * piece_wide]

    def to_right(block, piece):
        return remote(
            right_send.at[block, piece],
            from_left.at[block, piece],
            r_send.at[block, piece],
            r_recv.at[block, piece],
            {"rows": row + 1},
        )

    def to_left(block, piece):
        return remote(
            left_send.at[block, piece],
            from_right.at[block, piece],
            l_send.at[block, piece],
            l_recv.at[block, piece],
            {"rows": row - 1},
        )

    def run(move, send, arrived, block, edge):
        for piece in range(pieces):

            @pl.when(row == edge)
            def _():
                send[block, piece] = term(block, piece).astype(BF16)

            @pl.when(row != edge)
            def _():
                move(block, piece).wait_recv()
                send[block, piece] = (
                    term(block, piece) + arrived[block, piece].astype(F32)
                ).astype(BF16)

            move(block, piece).start()

    def run_right(block):
        run(to_right, right_send, from_left, block, 0)

    def run_left(block):
        run(to_left, left_send, from_right, block, row_count - 1)

    def send_far(from_end):
        at_end = (row == 0) | (row == row_count - 1)
        now = at_end if from_end else jnp.logical_not(at_end)

        @pl.when(now & (row < near))
        def _():
            each(near, lambda step: run_right(row_count - 1 - step))

        @pl.when(now & (row >= near))
        def _():
            each(near, run_left)

    near_chunks(stages[0], True)
    far_chunks(stages[0], True)
    send_far(True)
    if joint is not None:
        joint(home)
        share(stages[1])
        share(stages[2])
    near_chunks(stages[1], False)
    if has_up:
        far_chunks(stages[1], False)
        send_far(False)
        near_chunks(stages[2], False)
    else:
        far_chunks(stages[1], False)
        near_chunks(stages[2], False)
        send_far(False)

    @pl.when(row < pair)
    def _():
        run_right(pair)

    @pl.when(row > pair)
    def _():
        run_left(pair)

    far_chunks(stages[2], False)
    for piece in range(pieces):
        columns = slice(piece * piece_wide, (piece + 1) * piece_wide)
        total = term(row, piece) + base[:, columns].astype(F32)
        if has_up:
            total += bias[columns].reshape(1, -1)
        accum[row, :, columns] = total

        @pl.when(row > 0)
        def _():
            to_right(row, piece).wait_recv()
            accum[row, :, columns] += from_left[row, piece].astype(F32)

        @pl.when(row < row_count - 1)
        def _():
            to_left(row, piece).wait_recv()
            accum[row, :, columns] += from_right[row, piece].astype(F32)

        result[:, columns] = term(row, piece).astype(BF16)

    def sent(block):
        for piece in range(pieces):

            @pl.when(row < block)
            def _():
                to_right(block, piece).wait_send()

            @pl.when(row > block)
            def _():
                to_left(block, piece).wait_send()

    each(row_count, sent)

    for to_across, to_mate, forward, count in moves:

        def finish(unit):
            for half in stages:
                to_across(unit, half).wait_send()
                to_mate(unit, half).wait_send()
                forward(unit, half).wait_send()

        each(count, finish)


def out_scratch(groups, own_rows, width, row_count):
    dma = pltpu.SemaphoreType.DMA
    piece_wide = up_tile(width)
    pieces = width // piece_wide
    block = pltpu.VMEM((row_count, pieces, own_rows, piece_wide), BF16)
    scratch = [pltpu.VMEM((row_count, own_rows, width), F32)] + [block] * 4 + [dma((row_count, pieces))] * 4
    for count, piece in groups:
        scratch += [
            pltpu.VMEM((4 * count, piece, width), BF16),
            dma((4 * count,)),
            pltpu.VMEM((3, count, row_count, own_rows, piece), BF16),
            dma((count, 3)),
            dma((count, 3)),
            dma((count, 3)),
            dma((count, 3)),
            dma((2, count, 3)),
        ]
    return scratch


def out_call(name, number, base, heads, w_out, up=None):
    own_rows, width = base.shape
    _, half_rows, wide = heads.shape
    row_count = lax.axis_size("rows")
    any_spec, vmem_spec = pl.BlockSpec(memory_space=pl.ANY), pl.BlockSpec(memory_space=pltpu.VMEM)
    row_count = lax.axis_size("rows")
    operands = [base, heads.reshape(1, row_count, own_rows, wide), w_out]
    in_specs = [vmem_spec, vmem_spec, any_spec]
    groups = [(1, wide)]
    if up is not None:
        bias, hidden, w_down = up
        operands += [bias, hidden.reshape(hidden.shape[0], row_count, own_rows, -1), w_down]
        in_specs += [vmem_spec, vmem_spec, any_spec]
        groups.append((hidden.shape[0], hidden.shape[3]))
    scratch = out_scratch(groups, own_rows, width, row_count)
    return pl.pallas_call(
        functools.partial(out_kernel, up is not None),
        name=name,
        out_shape=jax.ShapeDtypeStruct((own_rows, width), BF16),
        in_specs=in_specs,
        out_specs=vmem_spec,
        scratch_shapes=scratch,
        compiler_params=pltpu.CompilerParams(
            collective_id=number, has_side_effects=True, vmem_limit_bytes=VMEM_LIMIT
        ),
    )(*operands)


def up_tile(columns):
    for tile in (4 * HEAD_DIM, 2 * HEAD_DIM, HEAD_DIM):
        if columns % tile == 0:
            return tile
    return columns


def kernel_body(
    camera_tokens,
    norm_gain,
    query_weight,
    key_weight,
    value_weight,
    query_gain,
    key_gain,
    out_weight,
    up_weight,
    up_bias,
    down_weight,
    down_bias,
    join_gain,
    join_query,
    join_key,
    join_value,
    join_query_gain,
    join_key_gain,
    join_out,
):
    all_rows = camera_tokens.shape[0] * lax.axis_size("rows")
    heads, hidden = in_call(
        "camera_in",
        0,
        TOK_CAM,
        camera_tokens,
        norm_gain,
        query_gain,
        key_gain,
        (query_weight, key_weight, value_weight),
        (up_bias, up_weight),
    )
    layer_own = out_call(
        "camera_out", 1, camera_tokens, heads, out_weight, (down_bias, hidden, down_weight)
    )
    return in_call(
        "join",
        2,
        all_rows,
        layer_own,
        join_gain,
        join_query_gain,
        join_key_gain,
        (join_query, join_key, join_value),
        join=join_out,
    )


def fits(mesh):
    cols, rows = mesh.shape["cols"], mesh.shape["rows"]
    return cols == 4 and rows == 4 and D % (rows * cols * HEAD_DIM) == 0


def solution(mesh):
    in_specs = (
        P(("groups", "rows"), "cols"),
        P("cols"),
        P("cols", "rows"),
        P("cols", "rows"),
        P("cols", "rows"),
        P("rows"),
        P("rows"),
        P("rows", "cols"),
        P("cols", "rows"),
        P("rows"),
        P("rows", "cols"),
        P("cols"),
        P("cols"),
        P("cols", "rows"),
        P("cols", "rows"),
        P("cols", "rows"),
        P("rows"),
        P("rows"),
        P("rows", "cols"),
    )
    out_specs = P(("groups", "rows"), "cols")
    body = kernel_body if fits(mesh) else plain_body
    return jax.shard_map(body, mesh=mesh, in_specs=in_specs, out_specs=out_specs, check_vma=False)
```

profile of v0, /device:TPU:0, one launch (start us, length us, event | category | flops | bytes accessed | tf_op | source)
XLA Modules:
  0.0 228.3 jit_solution(3661045645240443519)
XLA Ops:
  0.0 74.7 %camera_in.1 = (bf16[2,256,384]{2,1,0:T(8,128)(2,1)}, bf16[3,2,256,512]{3,2,1,0:T(8,128)(2,1)}) custom-call(bf16[128,1536]{1,0:T(8,128)(2,1)} %refs_0_.3, f32[1536]{0:T(1024)} %refs_1_.1, f32[1536]{0:T(1024)} %refs_2_.2, f32[1536]{0:T(1024)} %refs_3_.2, bf16[1536,1536]{1,0:T(8,128)(2,1)} %refs_4_.1, bf16[1536,1536]{1,0:T(8,128)(2,1)} %refs_5_.2, ...), custom_call_target="tpu_custom_call" | custom-call | tf_op jit(solution)/shard_map/camera_in/pallas_call | solution.py:607
  74.7 62.9 %camera_out.1.tokens = bf16[128,1536]{1,0:T(8,128)(2,1)} custom-call(bf16[128,1536]{1,0:T(8,128)(2,1)} %refs_0_.3, bf16[1,4,128,384]{3,2,1,0:T(8,128)(2,1)} %bitcast.4, bf16[1536,1536]{1,0:T(8,128)(2,1)} %refs_2_.3, f32[1536]{0:T(1024)} %refs_3_.3, bf16[3,4,128,512]{3,2,1,0:T(8,128)(2,1)} %bitcast.3, bf16[6144,1536]{1,0:T(8,128)(2,1)} %refs_5_.3), custom_call_target="tpu_custom_call" | custom-call | tf_op jit(solution)/shard_map/camera_out/pallas_call | solution.py:937
  137.6 89.0 %join.1 = bf16[128,1536]{1,0:T(8,128)(2,1)} custom-call(bf16[128,1536]{1,0:T(8,128)(2,1)} %camera_out.1.tokens, f32[1536]{0:T(1024)} %gain.1, f32[1536]{0:T(1024)} %q_gain.1, f32[1536]{0:T(1024)} %k_gain.1, bf16[1536,1536]{1,0:T(8,128)(2,1)} %wq.1, bf16[1536,1536]{1,0:T(8,128)(2,1)} %wk.1, bf16[1536,1536]{1,0:T(8,128)(2,1)} %wv.1, bf16[1536,1536]{1,0:T(8,128)(2,1)} %w_out.1), custom_call_target="tpu_custom_call" | custom-call | tf_op jit(solution)/shard_map/join/pallas_call | solution.py:596
  226.6 1.8 copy.21
where the time goes:
time: 229 us; the launch traced here: 228 us
  Pallas kernels  227 us (99%)
    pallas_call x1, Pallas kernels, in_call(): pl.pallas_call(functools.partial(join_kernel, span, float(depth * cols)),...  89 us
    pallas_call x1, Pallas kernels, in_call(): pl.pallas_call(functools.partial(in_kernel, span, up is not None, float(d...  74.7 us
    pallas_call x1, Pallas kernels, out_call(): pl.pallas_call(functools.partial(out_kernel, up is not None), name=name,...  62.9 us

commit v1 on v0

v1 whole, which is shorter than its diff:
```python
import functools
import math
import types

import jax
import jax.numpy as jnp
from jax import lax
from jax.experimental import pallas as pl
from jax.experimental.pallas import tpu as pltpu
from jax.sharding import PartitionSpec as P

HEAD_DIM = 128
TOK_CAM = 64
D = 6144


EPS = 1e-06


def partner_2(array, axis, bit):
    return lax.ppermute(array, axis, [(i, i ^ 1 << bit) for i in range(lax.axis_size(axis))])


def normalize(values, scales, moments):
    row_mean = moments[0] / D
    row_var = moments[1] / D - row_mean * row_mean
    return ((values - row_mean[:, None]) * lax.rsqrt(row_var[:, None] + EPS) * scales).astype(
        jnp.bfloat16
    )


def shard_moments(values):
    return lax.psum((jnp.sum(values, 1), jnp.sum(values * values, 1)), "cols")


def head_norm(values, scales):
    row_count = values.shape[0]
    grouped = values.reshape(row_count, -1, HEAD_DIM)
    row_mean = jnp.mean(grouped, -1, keepdims=True)
    row_var = jnp.mean(grouped * grouped, -1, keepdims=True) - row_mean * row_mean
    normed = (grouped - row_mean) * lax.rsqrt(row_var + EPS)
    return (normed.reshape(row_count, -1) * scales).astype(jnp.bfloat16)


def attend(queries, key_rows, val_rows):
    inv_root = 1.0 / math.sqrt(HEAD_DIM)
    scores = (
        jnp.einsum("bqhd,bkhd->bhqk", queries, key_rows, preferred_element_type=jnp.float32)
        * inv_root
    )
    row_max = jnp.max(scores, -1, keepdims=True)
    weights = jnp.exp(scores - row_max)
    row_sum = jnp.sum(weights, -1)
    blended = jnp.einsum(
        "bhqk,bkhd->bqhd",
        weights.astype(jnp.bfloat16),
        val_rows,
        preferred_element_type=jnp.float32,
    )
    return blended / jnp.transpose(row_sum, (0, 2, 1))[..., None]


def to_heads(matrix, blocks):
    return matrix.reshape(blocks, -1, matrix.shape[1] // HEAD_DIM, HEAD_DIM)


def camera_attention(queries, key_rows, val_rows):
    local_rows = queries.shape[0]
    if local_rows >= TOK_CAM:
        blocks = local_rows // TOK_CAM
        result = attend(
            to_heads(queries, blocks), to_heads(key_rows, blocks), to_heads(val_rows, blocks)
        )
    else:
        cam_span = TOK_CAM // local_rows
        position = lax.axis_index("cols")
        key_value = jnp.stack((key_rows, val_rows))
        for which_bit in range(cam_span.bit_length() - 1):
            partner = partner_2(key_value, "cols", which_bit)
            is_lower = position >> which_bit & 1 == 0
            key_value = jnp.where(
                is_lower,
                jnp.concatenate((key_value, partner), 1),
                jnp.concatenate((partner, key_value), 1),
            )
        result = attend(to_heads(queries, 1), to_heads(key_value[0], 1), to_heads(key_value[1], 1))
    return result.reshape(local_rows, -1).astype(jnp.bfloat16)


def plain_body(
    camera_tokens,
    norm_gain,
    query_weight,
    key_weight,
    value_weight,
    query_gain,
    key_gain,
    out_weight,
    up_weight,
    up_bias,
    down_weight,
    down_bias,
    join_gain,
    join_query,
    join_key,
    join_value,
    join_query_gain,
    join_key_gain,
    join_out,
):
    own_rows = camera_tokens.shape[0]
    all_rows = own_rows * lax.axis_size("rows")
    col_rows = all_rows // lax.axis_size("cols")
    attn_width = query_weight.shape[1]
    start_f32 = camera_tokens.astype(jnp.float32)
    normed_all = lax.all_gather(
        normalize(start_f32, norm_gain, shard_moments(start_f32)), "rows", axis=0, tiled=True
    )
    joint_weight = jnp.concatenate((query_weight, key_weight, value_weight, up_weight), 1)
    joint = lax.psum_scatter(
        jnp.dot(normed_all, joint_weight, preferred_element_type=jnp.float32),
        "cols",
        scatter_dimension=0,
        tiled=True,
    )
    up_sum = joint[:, 3 * attn_width :]
    hidden = jax.nn.gelu(up_sum + up_bias, approximate=False).astype(jnp.bfloat16)
    attended = camera_attention(
        head_norm(joint[:, :attn_width], query_gain),
        head_norm(joint[:, attn_width : 2 * attn_width], key_gain),
        joint[:, 2 * attn_width : 3 * attn_width].astype(jnp.bfloat16),
    )
    attn_all, hidden_all = (
        lax.all_gather(attended, "cols", axis=0, tiled=True),
        lax.all_gather(hidden, "cols", axis=0, tiled=True),
    )
    mixed = lax.psum_scatter(
        jnp.dot(attn_all, out_weight, preferred_element_type=jnp.float32)
        + jnp.dot(hidden_all, down_weight, preferred_element_type=jnp.float32),
        "rows",
        scatter_dimension=0,
        tiled=True,
    )
    layer_own = (start_f32 + mixed + down_bias).astype(jnp.bfloat16)
    layer_f32 = layer_own.astype(jnp.float32)
    join_in = lax.all_gather(
        normalize(layer_f32, join_gain, shard_moments(layer_f32)), "rows", axis=0, tiled=True
    )
    join_weight = jnp.concatenate((join_query, join_key, join_value), 1)
    join_joint = lax.psum_scatter(
        jnp.dot(join_in, join_weight, preferred_element_type=jnp.float32),
        "cols",
        scatter_dimension=0,
        tiled=True,
    )
    join_q = head_norm(join_joint[:, :attn_width], join_query_gain)
    join_k = head_norm(join_joint[:, attn_width : 2 * attn_width], join_key_gain)
    join_v = join_joint[:, 2 * attn_width :].astype(jnp.bfloat16)
    heads_here = attn_width // HEAD_DIM
    query_heads = join_q.reshape(col_rows, heads_here, HEAD_DIM)
    inv_root = 1.0 / math.sqrt(HEAD_DIM)
    run_max = jnp.full((heads_here, col_rows), -jnp.inf, jnp.float32)
    run_sum = jnp.zeros((heads_here, col_rows), jnp.float32)
    accum = jnp.zeros((col_rows, heads_here, HEAD_DIM), jnp.float32)
    key_part = lax.all_gather(join_k, "cols", axis=0, tiled=True)
    val_part = lax.all_gather(join_v, "cols", axis=0, tiled=True)
    row_count = key_part.shape[0]
    key_heads = key_part.reshape(row_count, heads_here, HEAD_DIM)
    val_heads = val_part.reshape(row_count, heads_here, HEAD_DIM)
    scores = (
        jnp.einsum("qhd,khd->hqk", query_heads, key_heads, preferred_element_type=jnp.float32)
        * inv_root
    )
    new_max = jnp.max(scores, -1)
    factor = jnp.exp(run_max - new_max)
    weights = jnp.exp(scores - new_max[..., None])
    run_sum = run_sum * factor + jnp.sum(weights, -1)
    accum = accum * jnp.transpose(factor)[..., None] + jnp.einsum(
        "hqk,khd->qhd", weights.astype(jnp.bfloat16), val_heads, preferred_element_type=jnp.float32
    )
    run_max, run_sum, accum = (new_max, run_sum, accum)
    joined_attn = (
        (accum / jnp.transpose(run_sum)[..., None])
        .reshape(col_rows, attn_width)
        .astype(jnp.bfloat16)
    )
    joined_all = lax.all_gather(joined_attn, "cols", axis=0, tiled=True)
    result = lax.psum_scatter(
        jnp.dot(joined_all, join_out, preferred_element_type=jnp.float32),
        "rows",
        scatter_dimension=0,
        tiled=True,
    )
    return (layer_own.astype(jnp.float32) + result).astype(jnp.bfloat16)


F32 = jnp.float32
BF16 = jnp.bfloat16
MESH = pl.DeviceIdType.MESH
VMEM_LIMIT = 66 * 1024 * 1024 - 3 * 1024 * 1024


def each(count, step):
    lax.fori_loop(0, count, lambda i, carry: (step(i), carry)[1], None)


def remote(src, dst, send, recv, device):
    return pltpu.make_async_remote_copy(
        src_ref=src,
        dst_ref=dst,
        send_sem=send,
        recv_sem=recv,
        device_id=device,
        device_id_type=MESH,
    )


def places():
    col = lax.axis_index("cols")
    core = lax.rem(col, 2)
    return col, col + 1 - 2 * core, lax.rem(col + 2, 4)


def greet(cols_away):
    col, row, row_count = lax.axis_index("cols"), lax.axis_index("rows"), lax.axis_size("rows")
    barrier = pltpu.get_barrier_semaphore()
    _, mate, across = places()
    others = {1: mate, 2: across}
    if cols_away == 3:
        others[3] = mate + across - col
    for other in others.values():
        pl.semaphore_signal(barrier, inc=1, device_id={"cols": other}, device_id_type=MESH)

    @pl.when(row > 0)
    def _():
        pl.semaphore_signal(barrier, inc=1, device_id={"rows": row - 1}, device_id_type=MESH)

    @pl.when(row < row_count - 1)
    def _():
        pl.semaphore_signal(barrier, inc=1, device_id={"rows": row + 1}, device_id_type=MESH)

    inner = (row > 0) & (row < row_count - 1)

    @pl.when(inner)
    def _():
        pl.semaphore_wait(barrier, len(others) + 2)

    @pl.when(jnp.logical_not(inner))
    def _():
        pl.semaphore_wait(barrier, len(others) + 1)


def norm_heads(values, scales):
    parts = []
    for start in range(0, values.shape[1], HEAD_DIM):
        part = values[:, start : start + HEAD_DIM]
        mean = jnp.mean(part, -1, keepdims=True)
        var = jnp.mean(part * part, -1, keepdims=True) - mean * mean
        parts.append((part - mean) * lax.rsqrt(var + EPS))
    return (jnp.concatenate(parts, 1) * scales).astype(BF16)


def soft_blend(query, keys, values):
    scores = lax.dot_general(
        query, keys, (((1,), (1,)), ((), ())), preferred_element_type=F32
    ) * (1.0 / math.sqrt(HEAD_DIM))
    weights = jnp.exp(scores - jnp.max(scores, -1, keepdims=True))
    total = jnp.sum(weights, -1, keepdims=True)
    blended = jnp.dot(weights.astype(BF16), values, preferred_element_type=F32)
    return (blended / total).astype(BF16)


def layer_kernel(names, width, *refs):
    r = types.SimpleNamespace(**dict(zip(names, refs)))
    normed, accum, pool, pool_sem = r.normed, r.accum, r.pool, r.pool_sem
    col, mate, across = places()
    diagonal = mate + across - col
    owners = (col, mate, across, diagonal)
    row, rows = lax.axis_index("rows"), lax.axis_size("rows")
    chunks, _, piece, depth = normed.shape
    half = chunks // 2
    ups = r.f_send1.shape[0]
    tile = pool.shape[1]
    wide = r.hid0.shape[-1]
    out_pieces = accum.shape[-1] // tile
    in_pieces = depth // tile
    slot_pieces = max(in_pieces, out_pieces)
    n_in, n_out = 3 + ups, 1 + ups
    last = chunks - 1
    ring = 2 * n_in
    mine = pl.ds(pl.multiple_of(col * wide, HEAD_DIM), wide)
    own_place, mate_place, across_place, diag_place = range(4)

    def load_in(source, slot, start, wid):
        first = slot * slot_pieces
        return pltpu.make_async_copy(
            source.at[:, :, pl.ds(pl.multiple_of(start, HEAD_DIM), wid)],
            pool.at[pl.ds(first, in_pieces), :, pl.ds(0, wid)],
            pool_sem.at[first],
        )

    def load_out(source, slot, start, deep):
        for j in range(out_pieces):
            place = slot * slot_pieces + j
            pltpu.make_async_copy(
                source.at[pl.ds(pl.multiple_of(start, HEAD_DIM), deep), pl.ds(j * tile, tile)],
                pool.at[place, pl.ds(0, deep)],
                pool_sem.at[place],
            ).start()

    def load_camera_in(owner, slot):
        for which, source in enumerate((r.wq, r.wk, r.wv)):
            load_in(source, slot + which, owner * wide, wide).start()
        each(
            ups,
            lambda unit: load_in(
                r.w_up, slot + 3 + unit, owner * (ups * tile) + unit * tile, tile
            ).start(),
        )

    def load_join_in(owner, slot):
        for which, source in enumerate((r.jq, r.jk, r.jv)):
            load_in(source, slot + which, owner * wide, wide).start()

    def load_camera_out(owner, slot):
        load_out(r.w_out, slot, owner * wide, wide)
        each(ups, lambda unit: load_out(r.w_down, slot + 1 + unit, (owner * ups + unit) * tile, tile))

    def in_weight(slot, wid):
        first = slot * slot_pieces
        return pool.at[pl.ds(first, in_pieces), :, pl.ds(0, wid)], pool_sem.at[first]

    def wait_in(slot, wid):
        part, sem = in_weight(slot, wid)
        pltpu.make_async_copy(part, part, sem).wait()

    def wait_out(slot, deep):
        for j in range(out_pieces):
            place = slot * slot_pieces + j
            part = pool.at[place, pl.ds(0, deep)]
            pltpu.make_async_copy(part, part, pool_sem.at[place]).wait()

    def product(slot, left, wid):
        part, _ = in_weight(slot, wid)
        return jnp.dot(left, part[...].reshape(depth, wid), preferred_element_type=F32)

    def add_tile(span, value, slot, begin=False):
        start, count = span
        deep = value.shape[1]
        for j in range(out_pieces):
            part = jnp.dot(
                value, pool[slot * slot_pieces + j, pl.ds(0, deep)], preferred_element_type=F32
            ).reshape(count, rows, piece, tile)
            at = (pl.ds(start, count), slice(None), slice(None), slice(j * tile, (j + 1) * tile))
            if begin:
                accum[at] = part
            else:
                accum[at] += part

    def gather_copy(stage, span, block, right):
        rel = lax.rem(block - row + rows, rows)
        away = lax.rem(rel + (rows - 1 if right else 1), rows)
        part = pl.ds(*span)
        return remote(
            normed.at[part, rel],
            normed.at[part, away],
            (r.g_right if right else r.g_left).at[stage, block],
            r.g_arrive.at[stage, block],
            {"rows": row + 1 if right else row - 1},
        )

    def arrival(stage, span, block):
        rel = lax.rem(block - row + rows, rows)
        part = normed.at[pl.ds(*span), rel]
        pltpu.make_async_copy(part, part, r.g_arrive.at[stage, block]).wait()

    def pass_on(stage, span, block, right):
        @pl.when((row < rows - 1) if right else (row > 0))
        def _():
            gather_copy(stage, span, block, right).start()

    def spread(stage, span):
        pass_on(stage, span, row, True)
        pass_on(stage, span, row, False)

    def take(stage, span, away):
        @pl.when(row >= away)
        def _():
            arrival(stage, span, row - away)
            pass_on(stage, span, row - away, True)

        @pl.when(row + away < rows)
        def _():
            arrival(stage, span, row + away)
            pass_on(stage, span, row + away, False)

    def spread_done(stage, span):
        def done(block):
            @pl.when((row >= block) & (row < rows - 1))
            def _():
                gather_copy(stage, span, block, True).wait_send()

            @pl.when((row <= block) & (row > 0))
            def _():
                gather_copy(stage, span, block, False).wait_send()

        each(rows, done)

    f_send, f_recv, y_recv = (r.f_send0, r.f_send1), (r.f_recv0, r.f_recv1), (r.y_recv0, r.y_recv1)
    p_send, p_recv = (r.p_send0, r.p_send1), (r.p_recv0, r.p_recv1)
    first_sems = ((r.fs0, r.fr0, r.ys0, r.yr0), (r.fs1, r.fr1, r.ys1, r.yr1))
    second_sems = ((r.ps0, r.pr0), (r.ps1, r.pr1))
    counts, wides, offsets = (3, ups), (wide, tile), (0, 3)

    def left_of(region):
        c0, nc, r0, nr = region
        return normed[pl.ds(c0, nc), pl.ds(r0, nr)].reshape(nc * nr * piece, depth)

    def part_of(region):
        c0, nc, r0, nr = region
        return pl.ds(c0, nc), pl.ds(r0, nr)

    def shaped(value, region):
        return value.reshape(region[1], region[3], piece, value.shape[-1])

    def f_copy(group, unit, stage, region):
        at = (unit, *part_of(region))
        fs, fr, _, _ = first_sems[group]
        return remote(
            f_send[group].at[at],
            f_recv[group].at[at],
            fs.at[unit, stage],
            fr.at[unit, stage],
            {"cols": mate},
        )

    def y_copy(group, unit, stage, region):
        at = (unit, *part_of(region))
        _, _, ys, yr = first_sems[group]
        return remote(
            f_send[group].at[at],
            y_recv[group].at[at],
            ys.at[unit, stage],
            yr.at[unit, stage],
            {"cols": across},
        )

    def p_copy(group, unit, stage, span):
        at = (unit, pl.ds(*span))
        ps, pr = second_sems[group]
        return remote(
            p_send[group].at[at],
            p_recv[group].at[at],
            ps.at[unit, stage],
            pr.at[unit, stage],
            {"cols": mate},
        )

    def give(region, stage, groups, base, fresh):
        for group in groups:
            wid = wides[group]

            def step(unit):
                slot = base + offsets[group] + unit
                if fresh:
                    wait_in(slot, wid)
                value = product(slot, left_of(region), wid).astype(BF16)
                f_send[group][(unit, *part_of(region))] = shaped(value, region)
                f_copy(group, unit, stage, region).start()

            each(counts[group], step)

    def send(region, stage, groups, base, fresh):
        for group in groups:
            wid = wides[group]

            def step(unit):
                slot = base + offsets[group] + unit
                if fresh:
                    wait_in(slot, wid)
                value = shaped(product(slot, left_of(region), wid), region)
                at = (unit, *part_of(region))
                f_copy(group, unit, stage, region).wait()
                f_send[group][at] = (value + f_recv[group][at].astype(F32)).astype(BF16)
                y_copy(group, unit, stage, region).start()

            each(counts[group], step)

    def give_second(span, stage, groups, base, fresh):
        for group in groups:
            wid = wides[group]

            def step(unit):
                slot = base + offsets[group] + unit
                if fresh is True:
                    wait_in(slot, wid)
                elif fresh is not False:

                    @pl.when(fresh)
                    def _():
                        wait_in(slot, wid)

                region = (*span, 0, rows)
                value = product(slot, left_of(region), wid).astype(BF16)
                p_send[group][unit, pl.ds(*span)] = shaped(value, region)
                p_copy(group, unit, stage, span).start()

            each(counts[group], step)

    def final(group, unit, span, slot):
        region = (*span, 0, rows)
        wid = wides[group]
        part = pl.ds(*span)
        value = product(slot, left_of(region), wid)
        height = value.shape[0]
        got = p_recv[group][unit, part].astype(F32) + y_recv[group][unit, part].astype(F32)
        return value + got.reshape(height, wid)

    def final_qkv(span, base, gains, wait):
        region = (*span, 0, rows)
        for which in range(3):
            wait(which)
            value = final(0, which, span, base + which)
            if which < 2:
                value = norm_heads(value, gains[which][mine].reshape(1, -1))
            else:
                value = value.astype(BF16)
            r.qkv[which, pl.ds(*span)] = shaped(value, region)

    def hid(place, k, span):
        if isinstance(k, int) and k == 0:
            return r.hid0.at[place, pl.ds(*span)]
        return r.hid1.at[place, k - 1, pl.ds(*span)]

    def hid_value(place, k, span):
        part = hid(place, k, span)
        return part[...].reshape(span[1] * rows * piece, part.shape[-1])

    def tile_id(phase, k):
        return n_out if phase else k

    def to_across(phase, k, c):
        i = tile_id(phase, k)
        return remote(
            hid(own_place, k, (c, 1)),
            hid(across_place, k, (c, 1)),
            r.a_send.at[i, c],
            r.a_recv.at[i, c],
            {"cols": across},
        )

    def to_mate(phase, k, c):
        i = tile_id(phase, k)
        return remote(
            hid(own_place, k, (c, 1)),
            hid(mate_place, k, (c, 1)),
            r.b_send.at[i, c],
            r.b_recv.at[i, c],
            {"cols": mate},
        )

    def forward(phase, k, c):
        i = tile_id(phase, k)
        return remote(
            hid(across_place, k, (c, 1)),
            hid(diag_place, k, (c, 1)),
            r.d_send.at[i, c],
            r.d_recv.at[i, c],
            {"cols": mate},
        )

    def z_right(phase, c, rel):
        return remote(
            r.z_send.at[c, rel],
            r.z_left.at[c, rel - 1],
            r.zr_send.at[phase, c, rel],
            r.zr_recv.at[phase, c, rel - 1],
            {"rows": row + 1},
        )

    def z_left(phase, c, rel):
        there = (rel + 1) % rows
        return remote(
            r.z_send.at[c, rel],
            r.z_right.at[c, there],
            r.zl_send.at[phase, c, rel],
            r.zl_recv.at[phase, c, there],
            {"rows": row - 1},
        )

    def sums(phase, c, step):
        @pl.when(row == step)
        def _():
            for block in range(rows - 1, step, -1):
                rel = block - step
                value = accum[c, rel]
                if step > 0:
                    z_right(phase, c, rel + 1).wait_recv()
                    value += r.z_left[c, rel].astype(F32)
                r.z_send[c, rel] = value.astype(BF16)
                z_right(phase, c, rel).start()

        here = rows - 1 - step

        @pl.when(row == here)
        def _():
            for block in range(here):
                rel = block - here + rows
                value = accum[c, rel]
                if step > 0:
                    z_left(phase, c, rel - 1).wait_recv()
                    value += r.z_right[c, rel].astype(F32)
                r.z_send[c, rel] = value.astype(BF16)
                z_left(phase, c, rel).start()

    def sums_end(phase, c):
        @pl.when(row > 0)
        def _():
            z_right(phase, c, 1).wait_recv()
            accum[c, 0] += r.z_left[c, 0].astype(F32)

        @pl.when(row < rows - 1)
        def _():
            z_left(phase, c, rows - 1).wait_recv()
            accum[c, 0] += r.z_right[c, 0].astype(F32)

    def sums_sent(phase):
        def done(c):
            for rel in range(1, rows):

                @pl.when(row + rel < rows)
                def _():
                    z_right(phase, c, rel).wait_send()

                @pl.when(row + rel >= rows)
                def _():
                    z_left(phase, c, rel).wait_send()

        each(chunks, done)

    def swap(phase, stage, slot, part):
        other = (mate, across, diagonal)[slot]
        return remote(
            r.moments.at[phase, 3, part],
            r.moments.at[phase, slot, part],
            r.m_send.at[stage, slot],
            r.m_recv.at[stage, slot],
            {"cols": other},
        )

    def moments_start(phase, stage, part, values):
        count = values.shape[0]
        flat = values.reshape(count * piece, depth)
        lane = lax.broadcasted_iota(jnp.int32, (count * piece, HEAD_DIM), 1)
        pair = jnp.where(
            lane < HEAD_DIM // 2,
            jnp.sum(flat, 1, keepdims=True),
            jnp.sum(flat * flat, 1, keepdims=True),
        )
        r.moments[phase, 3, part] = pair.reshape(count, piece, HEAD_DIM)
        for slot in range(3):
            swap(phase, stage, slot, part).start()

    def moments_end(phase, stage, part, values, gain):
        for slot in range(3):
            swap(phase, stage, slot, part).wait_recv()
        m = r.moments
        total = (m[phase, 3, part] + m[phase, 0, part]) + (m[phase, 1, part] + m[phase, 2, part])
        mean = total[:, :, :1] / width
        var = total[:, :, HEAD_DIM // 2 : HEAD_DIM // 2 + 1] / width - mean * mean
        scaled = (values - mean) * lax.rsqrt(var + EPS) * gain[...].reshape(1, 1, -1)
        normed[part, 0] = scaled.astype(BF16)

    def moments_sent(phase, stage, part):
        for slot in range(3):
            swap(phase, stage, slot, part).wait_send()

    load_camera_in(diagonal, 0)
    load_camera_in(across, n_in)
    load_camera_in(mate, ring)
    greet(3)
    every = pl.ds(0, chunks)
    halves = ((0, half), (half, half))
    own = r.tokens[...].astype(F32)
    moments_start(0, 0, every, own)
    moments_end(0, 0, every, own, r.gain)
    spread(0, halves[0])
    both = (0, 1)
    region = (0, chunks, 0, 1)
    give(region, 0, both, 0, True)
    take(0, halves[0], 1)
    send(region, 0, both, n_in, True)
    take(0, halves[0], 2)
    spread(1, halves[1])
    take(0, halves[0], 3)

    def others(h):
        rest = (h * half, half, 1, rows - 1)
        give(rest, 1 + h, both, 0, False)
        send(rest, 1 + h, both, n_in, False)

        @pl.when(h == 0)
        def _():
            take(1, halves[1], 1)

        give_second((h * half, half), h, both, ring, h == 0)

        @pl.when(h == 0)
        def _():
            take(1, halves[1], 2)
            take(1, halves[1], 3)

    each(2, others)
    load_camera_in(col, ring)
    load_camera_out(col, 0)
    load_camera_out(mate, n_out)
    load_camera_out(across, 2 * n_out)
    moments_sent(0, 0, every)
    for h in range(2):
        spread_done(h, halves[h])

    def share(phase, k, c, away):
        to_mate(phase, k, c).start()
        if away:
            to_across(phase, k, c).start()

    def finals(h):
        span = (h * half, half)
        rest = (h * half, half, 1, rows - 1)

        def arrived(group, unit):
            @pl.when(h == 0)
            def _():
                wait_in(ring + offsets[group] + unit, wides[group])
                y_copy(group, unit, 0, region).wait_recv()

            p_copy(group, unit, h, span).wait_recv()
            y_copy(group, unit, 1 + h, rest).wait_recv()

        final_qkv(span, ring, (r.q_gain, r.k_gain), lambda which: arrived(0, which))

        def camera(rel):
            for start in range(0, wide, HEAD_DIM):
                head = pl.ds(start, HEAD_DIM)
                q, k, v = (
                    r.qkv[which, pl.ds(*span), rel, :, head].reshape(half * piece, HEAD_DIM)
                    for which in range(3)
                )
                r.hid0[own_place, pl.ds(*span), rel, :, head] = soft_blend(q, k, v).reshape(
                    half, piece, HEAD_DIM
                )

        each(rows, camera)

        def ship(k):
            def one(i):
                c = h * half + i
                to_mate(0, k, c).start()

                @pl.when(h == 0)
                def _():
                    to_across(0, k, c).start()

            each(half, one)

        ship(0)

        def activate(unit):
            arrived(1, unit)
            raw = final(1, unit, span, ring + 3 + unit) + r.bias[col * ups + unit]
            value = (raw * (1.0 + lax.erf(raw * math.sqrt(0.5))) * 0.5).astype(BF16)
            r.hid1[own_place, unit, pl.ds(*span)] = shaped(value, (*span, 0, rows))
            ship(unit + 1)

        each(ups, activate)

        def fresh_out(slot, deep):
            @pl.when(h == 0)
            def _():
                wait_out(slot, deep)

        def arrived_mate(k):
            each(half, lambda i: to_mate(0, k, h * half + i).wait_recv())

        def near_up(place):
            def one(unit):
                slot = place * n_out + 1 + unit
                fresh_out(slot, tile)
                if place == mate_place:
                    arrived_mate(unit + 1)
                add_tile(span, hid_value(place, unit + 1, span), slot)

            return one

        fresh_out(0, wide)
        add_tile(span, hid_value(own_place, 0, span), 0, True)
        each(ups, near_up(own_place))
        fresh_out(n_out, wide)
        arrived_mate(0)
        add_tile(span, hid_value(mate_place, 0, span), n_out)
        each(ups, near_up(mate_place))

    each(2, finals)
    load_camera_out(diagonal, ring)
    load_join_in(diagonal, 0)
    load_join_in(across, 3)
    join_out_slots = (2 * n_out - 2, 2 * n_out - 1, ring + n_out, ring + n_out + 1)
    for place in range(4):
        load_out(r.w_join, join_out_slots[place], owners[place] * wide, wide)

    def far(c, k):
        ahead = k + AHEAD
        later, kind = c + ahead // n_out, ahead % n_out

        @pl.when((later >= half) & (later < chunks))
        def _():
            to_across(0, kind, later).start()

        to_across(0, k, c).wait_recv()
        forward(0, k, c).start()

        @pl.when(c == 0)
        def _():
            wait_out(2 * n_out + k, wide if k == 0 else tile)
            wait_out(ring + k, wide if k == 0 else tile)

        add_tile((c, 1), hid_value(across_place, k, (c, 1)), 2 * n_out + k)
        forward(0, k, c).wait_recv()
        add_tile((c, 1), hid_value(diag_place, k, (c, 1)), ring + k)

    def norm_start(c):
        sums_end(0, c)
        total = accum[c, 0] + r.tokens[c].astype(F32) + r.down_bias[...].reshape(1, -1)
        layer = total.astype(BF16)
        r.layer[c] = layer
        moments_start(1, 1 + c, pl.ds(c, 1), layer.astype(F32)[None])

    def norm_end(c):
        moments_end(1, 1 + c, pl.ds(c, 1), r.layer[pl.ds(c, 1)].astype(F32), r.join_gain)
        spread(2 + c, (c, 1))

    def steps(c):
        def before(back, action):
            @pl.when(c >= back)
            def _():
                action(c - back)

        far(c, 0)
        before(1, lambda b: sums(0, b, 1))
        far(c, 1)
        before(1, lambda b: sums(0, b, 2))
        for k in range(2, n_out):
            far(c, k)
            if k == 2:
                before(1, norm_start)
        sums(0, c, 0)
        before(1, norm_end)
        for away in range(1, rows):
            before(2, lambda b: take(2 + b, (b, 1), away))

    each(chunks, steps)
    load_join_in(mate, 2 * n_out)
    load_join_in(col, ring)

    def shared(c):
        for k in range(n_out):
            to_across(0, k, c).wait_send()
            to_mate(0, k, c).wait_send()
            forward(0, k, c).wait_send()

    each(chunks, shared)
    for group in range(2):

        def sent(unit):
            y_copy(group, unit, 0, region).wait_send()
            for h in range(2):
                y_copy(group, unit, 1 + h, (h * half, half, 1, rows - 1)).wait_send()
                p_copy(group, unit, h, (h * half, half)).wait_send()

        each(counts[group], sent)

    spans = [(last - 1, 1), (last, 1)]
    if chunks > 2:
        spans.insert(0, (0, last - 1))
    regions = [(*span, 0, rows) for span in spans]
    n_spans = len(spans)

    def join_give(i, fresh=False):
        give(regions[i], 3 + i, (0,), 0, fresh)

    def join_send(i, fresh=False):
        send(regions[i], 3 + i, (0,), 3, fresh)

    def join_second(i, fresh=False):
        give_second(spans[i], 2 + i, (0,), 2 * n_out, fresh)

    def join_final(i, fresh=False):
        def arrived(which):
            if fresh:
                wait_in(ring + which, wide)
            p_copy(0, which, 2 + i, spans[i]).wait_recv()
            y_copy(0, which, 3 + i, regions[i]).wait_recv()

        final_qkv(spans[i], ring, (r.jq_gain, r.jk_gain), arrived)

    def take_one(c, away):
        take(2 + c, (c, 1), away)

    main = n_spans == 3
    if main:
        join_give(0, True)
    sums(0, last, 1)
    take_one(last - 1, 1)
    if main:
        join_send(0, True)
    sums(0, last, 2)
    take_one(last - 1, 2)
    if main:
        join_second(0, True)
    norm_start(last)
    take_one(last - 1, 3)
    join_give(n_spans - 2, not main)
    join_send(n_spans - 2, not main)
    norm_end(last)
    join_second(n_spans - 2, not main)
    if main:
        join_final(0, True)
    take_one(last, 1)
    take_one(last, 2)
    join_final(n_spans - 2, not main)
    take_one(last, 3)
    join_give(n_spans - 1)
    join_send(n_spans - 1)
    join_second(n_spans - 1)
    sums_sent(0)
    join_final(n_spans - 1)

    def blend(c):
        for start in range(0, wide, HEAD_DIM):
            head = pl.ds(start, HEAD_DIM)
            q = r.qkv[0, c, :, :, head].reshape(rows * piece, HEAD_DIM)
            k, v = (
                r.qkv[which, :, :, :, head].reshape(chunks * rows * piece, HEAD_DIM)
                for which in (1, 2)
            )
            r.hid0[own_place, c, :, :, head] = soft_blend(q, k, v).reshape(rows, piece, HEAD_DIM)
        to_across(1, 0, c).start()
        to_mate(1, 0, c).start()

    def result_of(c):
        sums_end(1, c)
        r.result[c] = (accum[c, 0] + r.layer[c].astype(F32)).astype(BF16)

    lead = min(2, chunks)
    each(lead, blend)
    for slot in join_out_slots:
        wait_out(slot, wide)

    def join_steps(c):
        def add(place, begin=False):
            add_tile((c, 1), hid_value(place, 0, (c, 1)), join_out_slots[place], begin)

        @pl.when(c + lead < chunks)
        def _():
            blend(c + lead)

        add(own_place, True)
        to_mate(1, 0, c).wait_recv()
        add(mate_place)
        to_across(1, 0, c).wait_recv()
        forward(1, 0, c).start()
        add(across_place)
        forward(1, 0, c).wait_recv()
        add(diag_place)
        sums(1, c, 0)

        @pl.when(c >= 1)
        def _():
            sums(1, c - 1, 1)
            sums(1, c - 1, 2)

        @pl.when(c >= 2)
        def _():
            result_of(c - 2)

    each(chunks, join_steps)
    sums(1, last, 1)
    sums(1, last, 2)
    result_of(last - 1)
    result_of(last)

    sums_sent(1)

    def drained(c):
        to_across(1, 0, c).wait_send()
        to_mate(1, 0, c).wait_send()
        forward(1, 0, c).wait_send()
        moments_sent(1, 1 + c, pl.ds(c, 1))
        spread_done(2 + c, (c, 1))

    each(chunks, drained)
    for i in range(n_spans):

        def sent_join(unit):
            y_copy(0, unit, 3 + i, regions[i]).wait_send()
            p_copy(0, unit, 2 + i, spans[i]).wait_send()

        each(3, sent_join)


AHEAD = 3
CHUNKS = 4


def tile_of(depth, columns, cols):
    ups = 3
    tile = columns // cols // ups
    return ups, tile


def kernel_body(
    camera_tokens,
    norm_gain,
    query_weight,
    key_weight,
    value_weight,
    query_gain,
    key_gain,
    out_weight,
    up_weight,
    up_bias,
    down_weight,
    down_bias,
    join_gain,
    join_query,
    join_key,
    join_value,
    join_query_gain,
    join_key_gain,
    join_out,
):
    own_rows, depth = camera_tokens.shape
    rows, cols = lax.axis_size("rows"), lax.axis_size("cols")
    width = out_weight.shape[1]
    wide = query_weight.shape[1] // cols
    ups, tile = tile_of(depth, up_weight.shape[1], cols)
    chunks, piece = CHUNKS, own_rows // CHUNKS
    n_in, n_out = 3 + ups, 1 + ups
    slot_pieces = max(depth, width) // tile

    def blocked(weight):
        return weight.reshape(depth // tile, tile, weight.shape[1])

    any_spec, vmem_spec = pl.BlockSpec(memory_space=pl.ANY), pl.BlockSpec(memory_space=pltpu.VMEM)
    inputs = {
        "tokens": (camera_tokens.reshape(chunks, piece, depth), vmem_spec),
        "gain": (norm_gain, vmem_spec),
        "q_gain": (query_gain, vmem_spec),
        "k_gain": (key_gain, vmem_spec),
        "bias": (up_bias.reshape(cols * ups, 1, tile), vmem_spec),
        "down_bias": (down_bias, vmem_spec),
        "join_gain": (join_gain, vmem_spec),
        "jq_gain": (join_query_gain, vmem_spec),
        "jk_gain": (join_key_gain, vmem_spec),
        "wq": (blocked(query_weight), any_spec),
        "wk": (blocked(key_weight), any_spec),
        "wv": (blocked(value_weight), any_spec),
        "w_up": (blocked(up_weight), any_spec),
        "w_out": (out_weight, any_spec),
        "w_down": (down_weight, any_spec),
        "jq": (blocked(join_query), any_spec),
        "jk": (blocked(join_key), any_spec),
        "jv": (blocked(join_value), any_spec),
        "w_join": (join_out, any_spec),
    }
    dma, vmem = pltpu.SemaphoreType.DMA, pltpu.VMEM
    scratch = {
        "pool": vmem((3 * n_in * slot_pieces, tile, tile), BF16),
        "pool_sem": dma((3 * n_in * slot_pieces,)),
        "normed": vmem((chunks, rows, piece, depth), BF16),
        "moments": vmem((2, 4, chunks, piece, HEAD_DIM), F32),
        "m_send": dma((1 + chunks, 3)),
        "m_recv": dma((1 + chunks, 3)),
        "g_right": dma((2 + chunks, rows)),
        "g_left": dma((2 + chunks, rows)),
        "g_arrive": dma((2 + chunks, rows)),
        "qkv": vmem((3, chunks, rows, piece, wide), BF16),
        "hid0": vmem((4, chunks, rows, piece, wide), BF16),
        "hid1": vmem((4, ups, chunks, rows, piece, tile), BF16),
        "accum": vmem((chunks, rows, piece, width), F32),
        "z_send": vmem((chunks, rows, piece, width), BF16),
        "z_left": vmem((chunks, rows, piece, width), BF16),
        "z_right": vmem((chunks, rows, piece, width), BF16),
        "layer": vmem((chunks, piece, width), BF16),
    }
    for name in ("zr_send", "zr_recv", "zl_send", "zl_recv"):
        scratch[name] = dma((2, chunks, rows))
    for name in ("a_send", "a_recv", "b_send", "b_recv", "d_send", "d_recv"):
        scratch[name] = dma((n_out + 1, chunks))
    for group, (count, wid) in enumerate(((3, wide), (ups, tile))):
        for name in ("f_send", "f_recv", "y_recv", "p_send", "p_recv"):
            scratch[name + str(group)] = vmem((count, chunks, rows, piece, wid), BF16)
        for name in ("fs", "fr", "ys", "yr", "ps", "pr"):
            scratch[name + str(group)] = dma((count, 6))
    names = (*inputs, "result", *scratch)
    joined = pl.pallas_call(
        functools.partial(layer_kernel, names, float(depth * cols)),
        name="layer",
        out_shape=jax.ShapeDtypeStruct((chunks, piece, width), BF16),
        in_specs=[spec for _, spec in inputs.values()],
        out_specs=vmem_spec,
        scratch_shapes=list(scratch.values()),
        compiler_params=pltpu.CompilerParams(
            collective_id=0, has_side_effects=True, vmem_limit_bytes=VMEM_LIMIT
        ),
    )(*[value for value, _ in inputs.values()])
    return joined.reshape(own_rows, width)


def fits(mesh):
    cols, rows = mesh.shape["cols"], mesh.shape["rows"]
    return cols == 4 and rows == 4 and D % (rows * cols * HEAD_DIM) == 0


def body(*arrays):
    tokens, up_weight = arrays[0], arrays[8]
    own_rows, depth = tokens.shape
    ups, tile = tile_of(depth, up_weight.shape[1], lax.axis_size("cols"))
    wide = arrays[2].shape[1] // lax.axis_size("cols")
    good = (
        own_rows == 2 * TOK_CAM
        and tile * ups * lax.axis_size("cols") == up_weight.shape[1]
        and tile % HEAD_DIM == 0
        and depth % tile == 0
        and arrays[7].shape[1] == depth
        and wide <= tile
        and wide % HEAD_DIM == 0
    )
    return kernel_body(*arrays) if good else plain_body(*arrays)


def solution(mesh):
    in_specs = (
        P(("groups", "rows"), "cols"),
        P("cols"),
        P("cols", "rows"),
        P("cols", "rows"),
        P("cols", "rows"),
        P("rows"),
        P("rows"),
        P("rows", "cols"),
        P("cols", "rows"),
        P("rows"),
        P("rows", "cols"),
        P("cols"),
        P("cols"),
        P("cols", "rows"),
        P("cols", "rows"),
        P("cols", "rows"),
        P("rows"),
        P("rows"),
        P("rows", "cols"),
    )
    out_specs = P(("groups", "rows"), "cols")
    inner = body if fits(mesh) else plain_body
    return jax.shard_map(inner, mesh=mesh, in_specs=in_specs, out_specs=out_specs, check_vma=False)
```

time: 229 us -> 240 us (1.048)
  Pallas kernels: 227 us -> 238 us
    pallas_call x3 -> x1, Pallas kernels: 227 us -> 238 us  [kernel_body(): pl.pallas_call(functools.partial(layer_kernel, names, float(depth * cols)...]
where the time goes in v1:
time: 240 us; the launch traced here: 239 us
  Pallas kernels  238 us (99%)
    pallas_call x1, Pallas kernels, kernel_body(): pl.pallas_call(functools.partial(layer_kernel, names, float(depth * cols)...  238 us

profile of v1, /device:TPU:0, one launch (start us, length us, event | category | flops | bytes accessed | tf_op | source)
XLA Modules:
  0.0 239.3 jit_solution(9951181276426033549)
XLA Ops:
  0.0 237.6 %layer.1 = bf16[4,32,1536]{2,1,0:T(8,128)(2,1)} custom-call(bf16[4,32,1536]{2,1,0:T(8,128)(2,1)} %bitcast.18, f32[1536]{0:T(1024)} %refs_1_.1, f32[1536]{0:T(1024)} %refs_2_.1, f32[1536]{0:T(1024)} %refs_3_.1, f32[12,1,512]{2,1,0:T(1,128)} %bitcast.19, f32[1536]{0:T(1024)} %refs_5_.1, f32[1536]{0:T(1024)} %refs_6_.1, f32[1536]{0:T(1024)} %refs_7_.1, ...), custom_call_target="tpu_custom_call" | custom-call | tf_op jit(solution)/shard_map/layer/pallas_call | solution.py:1106
  237.6 1.8 copy.21

commit v2 on v1

--- a/solution.py
+++ b/solution.py
@@ -296,16 +296,15 @@
         return pltpu.make_async_copy(
             source.at[:, :, pl.ds(pl.multiple_of(start, HEAD_DIM), wid)],
             pool.at[pl.ds(first, in_pieces), :, pl.ds(0, wid)],
-            pool_sem.at[first],
+            pool_sem.at[slot],
         )
 
     def load_out(source, slot, start, deep):
         for j in range(out_pieces):
-            place = slot * slot_pieces + j
             pltpu.make_async_copy(
                 source.at[pl.ds(pl.multiple_of(start, HEAD_DIM), deep), pl.ds(j * tile, tile)],
-                pool.at[place, pl.ds(0, deep)],
-                pool_sem.at[place],
+                pool.at[slot * slot_pieces + j, pl.ds(0, deep)],
+                pool_sem.at[slot],
             ).start()
 
     def load_camera_in(owner, slot):
@@ -327,22 +326,19 @@
         each(ups, lambda unit: load_out(r.w_down, slot + 1 + unit, (owner * ups + unit) * tile, tile))
 
     def in_weight(slot, wid):
-        first = slot * slot_pieces
-        return pool.at[pl.ds(first, in_pieces), :, pl.ds(0, wid)], pool_sem.at[first]
+        return pool.at[pl.ds(slot * slot_pieces, in_pieces), :, pl.ds(0, wid)]
 
     def wait_in(slot, wid):
-        part, sem = in_weight(slot, wid)
-        pltpu.make_async_copy(part, part, sem).wait()
+        part = in_weight(slot, wid)
+        pltpu.make_async_copy(part, part, pool_sem.at[slot]).wait()
 
     def wait_out(slot, deep):
-        for j in range(out_pieces):
-            place = slot * slot_pieces + j
-            part = pool.at[place, pl.ds(0, deep)]
-            pltpu.make_async_copy(part, part, pool_sem.at[place]).wait()
+        part = pool.at[pl.ds(slot * slot_pieces, out_pieces), pl.ds(0, deep)]
+        pltpu.make_async_copy(part, part, pool_sem.at[slot]).wait()
 
     def product(slot, left, wid):
-        part, _ = in_weight(slot, wid)
-        return jnp.dot(left, part[...].reshape(depth, wid), preferred_element_type=F32)
+        weight = in_weight(slot, wid)[...].reshape(depth, wid)
+        return jnp.dot(left, weight, preferred_element_type=F32)
 
     def add_tile(span, value, slot, begin=False):
         start, count = span
@@ -357,59 +353,55 @@
             else:
                 accum[at] += part
 
-    def gather_copy(stage, span, block, right):
+    def gather_copy(c, block, right):
         rel = lax.rem(block - row + rows, rows)
         away = lax.rem(rel + (rows - 1 if right else 1), rows)
-        part = pl.ds(*span)
         return remote(
-            normed.at[part, rel],
-            normed.at[part, away],
-            (r.g_right if right else r.g_left).at[stage, block],
-            r.g_arrive.at[stage, block],
+            normed.at[c, rel],
+            normed.at[c, away],
+            r.g_send.at[int(right)],
+            r.g_arrive.at[c, block],
             {"rows": row + 1 if right else row - 1},
         )
 
-    def arrival(stage, span, block):
-        rel = lax.rem(block - row + rows, rows)
-        part = normed.at[pl.ds(*span), rel]
-        pltpu.make_async_copy(part, part, r.g_arrive.at[stage, block]).wait()
-
-    def pass_on(stage, span, block, right):
+    def arrival(c, block):
+        part = normed.at[c, lax.rem(block - row + rows, rows)]
+        pltpu.make_async_copy(part, part, r.g_arrive.at[c, block]).wait()
+
+    def pass_on(c, block, right):
         @pl.when((row < rows - 1) if right else (row > 0))
         def _():
-            gather_copy(stage, span, block, right).start()
-
-    def spread(stage, span):
-        pass_on(stage, span, row, True)
-        pass_on(stage, span, row, False)
-
-    def take(stage, span, away):
+            gather_copy(c, block, right).start()
+
+    def spread(c):
+        pass_on(c, row, True)
+        pass_on(c, row, False)
+
+    def take(c, away):
         @pl.when(row >= away)
         def _():
-            arrival(stage, span, row - away)
-            pass_on(stage, span, row - away, True)
+            arrival(c, row - away)
+            pass_on(c, row - away, True)
 
         @pl.when(row + away < rows)
         def _():
-            arrival(stage, span, row + away)
-            pass_on(stage, span, row + away, False)
-
-    def spread_done(stage, span):
-        def done(block):
-            @pl.when((row >= block) & (row < rows - 1))
+            arrival(c, row + away)
+            pass_on(c, row + away, False)
+
+    def spread_done():
+        for place in range(rows):
+
+            @pl.when(row == place)
             def _():
-                gather_copy(stage, span, block, True).wait_send()
-
-            @pl.when((row <= block) & (row > 0))
-            def _():
-                gather_copy(stage, span, block, False).wait_send()
-
-        each(rows, done)
+                if place < rows - 1:
+                    all_sent(normed.at[:, pl.ds(0, place + 1)], r.g_send.at[1])
+                if place > 0:
+                    all_sent(normed.at[:, pl.ds(0, rows - place)], r.g_send.at[0])
 
     f_send, f_recv, y_recv = (r.f_send0, r.f_send1), (r.f_recv0, r.f_recv1), (r.y_recv0, r.y_recv1)
     p_send, p_recv = (r.p_send0, r.p_send1), (r.p_recv0, r.p_recv1)
-    first_sems = ((r.fs0, r.fr0, r.ys0, r.yr0), (r.fs1, r.fr1, r.ys1, r.yr1))
-    second_sems = ((r.ps0, r.pr0), (r.ps1, r.pr1))
+    first_sems = ((r.fs0, r.fr0, r.yr0), (r.fs1, r.fr1, r.yr1))
+    second_recv = (r.pr0, r.pr1)
     counts, wides, offsets = (3, ups), (wide, tile), (0, 3)
 
     def left_of(region):
@@ -425,87 +417,77 @@
 
     def f_copy(group, unit, stage, region):
         at = (unit, *part_of(region))
-        fs, fr, _, _ = first_sems[group]
+        fs, fr, _ = first_sems[group]
         return remote(
-            f_send[group].at[at],
-            f_recv[group].at[at],
-            fs.at[unit, stage],
-            fr.at[unit, stage],
-            {"cols": mate},
+            f_send[group].at[at], f_recv[group].at[at], fs.at[unit], fr.at[unit, stage], {"cols": mate}
         )
 
     def y_copy(group, unit, stage, region):
         at = (unit, *part_of(region))
-        _, _, ys, yr = first_sems[group]
+        yr = first_sems[group][2]
         return remote(
             f_send[group].at[at],
             y_recv[group].at[at],
-            ys.at[unit, stage],
+            r.ys.at[group],
             yr.at[unit, stage],
             {"cols": across},
         )
 
     def p_copy(group, unit, stage, span):
         at = (unit, pl.ds(*span))
-        ps, pr = second_sems[group]
         return remote(
             p_send[group].at[at],
             p_recv[group].at[at],
-            ps.at[unit, stage],
-            pr.at[unit, stage],
+            r.ps.at[group],
+            second_recv[group].at[unit, stage],
             {"cols": mate},
         )
 
-    def give(region, stage, groups, base, fresh):
-        for group in groups:
-            wid = wides[group]
-
-            def step(unit):
-                slot = base + offsets[group] + unit
-                if fresh:
-                    wait_in(slot, wid)
-                value = product(slot, left_of(region), wid).astype(BF16)
-                f_send[group][(unit, *part_of(region))] = shaped(value, region)
-                f_copy(group, unit, stage, region).start()
-
-            each(counts[group], step)
-
-    def send(region, stage, groups, base, fresh):
-        for group in groups:
-            wid = wides[group]
-
-            def step(unit):
-                slot = base + offsets[group] + unit
-                if fresh:
-                    wait_in(slot, wid)
-                value = shaped(product(slot, left_of(region), wid), region)
-                at = (unit, *part_of(region))
-                f_copy(group, unit, stage, region).wait()
-                f_send[group][at] = (value + f_recv[group][at].astype(F32)).astype(BF16)
+    def all_sent(source, sem):
+        pltpu.make_async_copy(source, source, sem).wait()
+
+    def give(region, stage, group, base, fresh):
+        wid = wides[group]
+
+        def step(unit):
+            slot = base + offsets[group] + unit
+            if fresh:
+                wait_in(slot, wid)
+            value = product(slot, left_of(region), wid).astype(BF16)
+            f_send[group][(unit, *part_of(region))] = shaped(value, region)
+            f_copy(group, unit, stage, region).start()
+
+        each(counts[group], step)
+
+    def send(region, stage, group, base, fresh, start=True):
+        wid = wides[group]
+
+        def step(unit):
+            slot = base + offsets[group] + unit
+            if fresh:
+                wait_in(slot, wid)
+            value = shaped(product(slot, left_of(region), wid), region)
+            at = (unit, *part_of(region))
+            f_copy(group, unit, stage, region).wait()
+            f_send[group][at] = (value + f_recv[group][at].astype(F32)).astype(BF16)
+            if start:
                 y_copy(group, unit, stage, region).start()
 
-            each(counts[group], step)
-
-    def give_second(span, stage, groups, base, fresh):
-        for group in groups:
-            wid = wides[group]
-
-            def step(unit):
-                slot = base + offsets[group] + unit
-                if fresh is True:
-                    wait_in(slot, wid)
-                elif fresh is not False:
-
-                    @pl.when(fresh)
-                    def _():
-                        wait_in(slot, wid)
-
-                region = (*span, 0, rows)
-                value = product(slot, left_of(region), wid).astype(BF16)
-                p_send[group][unit, pl.ds(*span)] = shaped(value, region)
-                p_copy(group, unit, stage, span).start()
-
-            each(counts[group], step)
+        each(counts[group], step)
+
+    def give_second(span, stage, group, base, fresh):
+        wid = wides[group]
+        region = (*span, 0, rows)
+
+        def step(unit):
+            slot = base + offsets[group] + unit
+            if fresh:
+                wait_in(slot, wid)
+            value = product(slot, left_of(region), wid).astype(BF16)
+            p_send[group][unit, pl.ds(*span)] = shaped(value, region)
+            p_copy(group, unit, stage, span).start()
+
+        each(counts[group], step)
 
     def final(group, unit, span, slot):
         region = (*span, 0, rows)
@@ -536,197 +518,252 @@
         part = hid(place, k, span)
         return part[...].reshape(span[1] * rows * piece, part.shape[-1])
 
-    def tile_id(phase, k):
-        return n_out if phase else k
+    def of(sems, phase, k, c):
+        wrap = sems.shape[1]
+        if phase:
+            return sems.at[c // wrap, c % wrap]
+        return sems.at[k, c % wrap]
+
+    def kind(k):
+        return 0 if isinstance(k, int) and k == 0 else 1
 
     def to_across(phase, k, c):
-        i = tile_id(phase, k)
         return remote(
             hid(own_place, k, (c, 1)),
             hid(across_place, k, (c, 1)),
-            r.a_send.at[i, c],
-            r.a_recv.at[i, c],
+            r.a_send.at[kind(k)],
+            of(r.a_recv, phase, k, c),
             {"cols": across},
         )
 
-    def to_mate(phase, k, c):
-        i = tile_id(phase, k)
+    def half_to_mate(k, h):
+        span = (h * half, half)
         return remote(
-            hid(own_place, k, (c, 1)),
-            hid(mate_place, k, (c, 1)),
-            r.b_send.at[i, c],
-            r.b_recv.at[i, c],
+            hid(own_place, k, span),
+            hid(mate_place, k, span),
+            r.b_send.at[kind(k)],
+            r.b_recv.at[k, h],
             {"cols": mate},
         )
 
+    def to_mate(c):
+        return remote(
+            hid(own_place, 0, (c, 1)),
+            hid(mate_place, 0, (c, 1)),
+            r.b_send.at[0],
+            of(r.b_recv, 1, 0, c),
+            {"cols": mate},
+        )
+
     def forward(phase, k, c):
-        i = tile_id(phase, k)
         return remote(
             hid(across_place, k, (c, 1)),
             hid(diag_place, k, (c, 1)),
-            r.d_send.at[i, c],
-            r.d_recv.at[i, c],
+            r.d_send.at[kind(k)],
+            of(r.d_recv, phase, k, c),
             {"cols": mate},
         )
 
-    def z_right(phase, c, rel):
+    def z_right(c, rel):
         return remote(
-            r.z_send.at[c, rel],
-            r.z_left.at[c, rel - 1],
-            r.zr_send.at[phase, c, rel],
-            r.zr_recv.at[phase, c, rel - 1],
+            r.z_send.at[c, rel - 1],
+            r.z_in.at[c, rel - 1],
+            r.z_sent.at[0],
+            r.z_arrive.at[c, rel - 1],
             {"rows": row + 1},
         )
 
-    def z_left(phase, c, rel):
-        there = (rel + 1) % rows
+    def z_left(c, rel):
+        there = (rel + 1) % rows or rows
         return remote(
-            r.z_send.at[c, rel],
-            r.z_right.at[c, there],
-            r.zl_send.at[phase, c, rel],
-            r.zl_recv.at[phase, c, there],
+            r.z_send.at[c, rel - 1],
+            r.z_in.at[c, there],
+            r.z_sent.at[0],
+            r.z_arrive.at[c, there],
             {"rows": row - 1},
         )
 
-    def sums(phase, c, step):
+    def z_wait(c, place):
+        part = r.z_in.at[c, place]
+        pltpu.make_async_copy(part, part, r.z_arrive.at[c, place]).wait()
+
+    def sums(c, step):
+        def go(rel, move):
+            value = accum[c, rel]
+            if step > 0:
+                z_wait(c, rel)
+                value += r.z_in[c, rel].astype(F32)
+            r.z_send[c, rel - 1] = value.astype(BF16)
+            move(c, rel).start()
+
         @pl.when(row == step)
         def _():
             for block in range(rows - 1, step, -1):
-                rel = block - step
-                value = accum[c, rel]
-                if step > 0:
-                    z_right(phase, c, rel + 1).wait_recv()
-                    value += r.z_left[c, rel].astype(F32)
-                r.z_send[c, rel] = value.astype(BF16)
-                z_right(phase, c, rel).start()
+                go(block - step, z_right)
 
         here = rows - 1 - step
 
         @pl.when(row == here)
         def _():
             for block in range(here):
-                rel = block - here + rows
-                value = accum[c, rel]
-                if step > 0:
-                    z_left(phase, c, rel - 1).wait_recv()
-                    value += r.z_right[c, rel].astype(F32)
-                r.z_send[c, rel] = value.astype(BF16)
-                z_left(phase, c, rel).start()
-
-    def sums_end(phase, c):
+                go(block - here + rows, z_left)
+
+    def sums_end(c):
         @pl.when(row > 0)
         def _():
-            z_right(phase, c, 1).wait_recv()
-            accum[c, 0] += r.z_left[c, 0].astype(F32)
+            z_wait(c, 0)
+            accum[c, 0] += r.z_in[c, 0].astype(F32)
 
         @pl.when(row < rows - 1)
         def _():
-            z_left(phase, c, rows - 1).wait_recv()
-            accum[c, 0] += r.z_right[c, 0].astype(F32)
-
-    def sums_sent(phase):
-        def done(c):
-            for rel in range(1, rows):
-
-                @pl.when(row + rel < rows)
-                def _():
-                    z_right(phase, c, rel).wait_send()
-
-                @pl.when(row + rel >= rows)
-                def _():
-                    z_left(phase, c, rel).wait_send()
-
-        each(chunks, done)
-
-    def swap(phase, stage, slot, part):
-        other = (mate, across, diagonal)[slot]
-        return remote(
-            r.moments.at[phase, 3, part],
-            r.moments.at[phase, slot, part],
-            r.m_send.at[stage, slot],
-            r.m_recv.at[stage, slot],
-            {"cols": other},
-        )
-
-    def moments_start(phase, stage, part, values):
-        count = values.shape[0]
-        flat = values.reshape(count * piece, depth)
-        lane = lax.broadcasted_iota(jnp.int32, (count * piece, HEAD_DIM), 1)
-        pair = jnp.where(
+            z_wait(c, rows)
+            accum[c, 0] += r.z_in[c, rows].astype(F32)
+
+    others = (mate, across, diagonal)
+
+    def pairs(flat):
+        lane = lax.broadcasted_iota(jnp.int32, (flat.shape[0], HEAD_DIM), 1)
+        return jnp.where(
             lane < HEAD_DIM // 2,
             jnp.sum(flat, 1, keepdims=True),
             jnp.sum(flat * flat, 1, keepdims=True),
         )
-        r.moments[phase, 3, part] = pair.reshape(count, piece, HEAD_DIM)
+
+    def normal(values, mean, square, gain):
+        var = square / width - mean * mean
+        return ((values - mean) * lax.rsqrt(var + EPS) * gain[...].reshape(1, -1)).astype(BF16)
+
+    def swap(c, slot):
+        i = c % half
+        return remote(
+            r.moments.at[3, c],
+            r.moments.at[slot, c],
+            r.m_send.at[i, slot],
+            r.m_recv.at[i, slot],
+            {"cols": others[slot]},
+        )
+
+    def norm_start(c):
+        sums_end(c)
+        total = accum[c, 0] + r.tokens[c].astype(F32) + r.down_bias[...].reshape(1, -1)
+        layer = total.astype(BF16)
+        r.layer[c] = layer
+        r.moments[3, c] = pairs(layer.astype(F32))
         for slot in range(3):
-            swap(phase, stage, slot, part).start()
-
-    def moments_end(phase, stage, part, values, gain):
+            swap(c, slot).start()
+
+    def norm_end(c):
         for slot in range(3):
-            swap(phase, stage, slot, part).wait_recv()
+            swap(c, slot).wait()
         m = r.moments
-        total = (m[phase, 3, part] + m[phase, 0, part]) + (m[phase, 1, part] + m[phase, 2, part])
-        mean = total[:, :, :1] / width
-        var = total[:, :, HEAD_DIM // 2 : HEAD_DIM // 2 + 1] / width - mean * mean
-        scaled = (values - mean) * lax.rsqrt(var + EPS) * gain[...].reshape(1, 1, -1)
-        normed[part, 0] = scaled.astype(BF16)
-
-    def moments_sent(phase, stage, part):
-        for slot in range(3):
-            swap(phase, stage, slot, part).wait_send()
+        total = (m[3, c] + m[0, c]) + (m[1, c] + m[2, c])
+        at = HEAD_DIM // 2
+        normed[c, 0] = normal(
+            r.layer[c].astype(F32), total[:, :1] / width, total[:, at : at + 1], r.join_gain
+        )
+        for place in range(rows):
+
+            @pl.when(row == place)
+            def _():
+                for there in range(rows):
+                    if abs(there - place) == 1 or (abs(there - place) == 2 and place in (0, rows - 1)):
+                        cast(c, place, there, place)
+
+    def cast(c, place, there, block):
+        rel, away = (block - place) % rows, (block - there) % rows
+        remote(
+            normed.at[c, rel],
+            normed.at[c, away],
+            r.g_send.at[2],
+            r.g_arrive.at[c, away],
+            {"rows": there},
+        ).start()
+
+    def landed(c, rel):
+        part = normed.at[c, rel]
+        pltpu.make_async_copy(part, part, r.g_arrive.at[c, rel]).wait()
+
+    def relay(c):
+        for place, there, blocks in ((1, 0, (2, 3)), (2, 3, (1, 0))):
+
+            @pl.when(row == place)
+            def _():
+                for block in blocks:
+                    landed(c, (block - place) % rows)
+                    cast(c, place, there, block)
+
+    def gathered(c):
+        for place in range(rows):
+
+            @pl.when(row == place)
+            def _():
+                for block in (((1, 2, 3), (0,), (3,), (2, 1, 0))[place]):
+                    landed(c, (block - place) % rows)
 
     load_camera_in(diagonal, 0)
     load_camera_in(across, n_in)
     load_camera_in(mate, ring)
     greet(3)
-    every = pl.ds(0, chunks)
-    halves = ((0, half), (half, half))
-    own = r.tokens[...].astype(F32)
-    moments_start(0, 0, every, own)
-    moments_end(0, 0, every, own, r.gain)
-    spread(0, halves[0])
-    both = (0, 1)
+    own = r.tokens[...].reshape(chunks * piece, depth).astype(F32)
+    few = r.start.shape[1]
+    begin = HEAD_DIM // 2 - few // 2
+    r.start[3] = jnp.transpose(pairs(own))[begin : begin + few]
+    swaps = [
+        remote(
+            r.start.at[3],
+            r.start.at[slot],
+            r.m_send.at[half, slot],
+            r.m_recv.at[half, slot],
+            {"cols": others[slot]},
+        )
+        for slot in range(3)
+    ]
+    for move in swaps:
+        move.start()
+    for move in swaps:
+        move.wait()
+    total = (r.start[3] + r.start[0]) + (r.start[1] + r.start[2])
+    total = jnp.transpose(jnp.concatenate([total] * (HEAD_DIM // few), 0))
+    normed[:, 0] = normal(
+        own, total[:, :1] / width, total[:, few // 2 : few // 2 + 1], r.gain
+    ).reshape(chunks, piece, depth)
+    first_half, second_half = (0, half), (half, half)
+    each(half, spread)
     region = (0, chunks, 0, 1)
-    give(region, 0, both, 0, True)
-    take(0, halves[0], 1)
-    send(region, 0, both, n_in, True)
-    take(0, halves[0], 2)
-    spread(1, halves[1])
-    take(0, halves[0], 3)
-
-    def others(h):
-        rest = (h * half, half, 1, rows - 1)
-        give(rest, 1 + h, both, 0, False)
-        send(rest, 1 + h, both, n_in, False)
-
-        @pl.when(h == 0)
-        def _():
-            take(1, halves[1], 1)
-
-        give_second((h * half, half), h, both, ring, h == 0)
-
-        @pl.when(h == 0)
-        def _():
-            take(1, halves[1], 2)
-            take(1, halves[1], 3)
-
-    each(2, others)
-    load_camera_in(col, ring)
+    rest = [(h * half, half, 1, rows - 1) for h in range(2)]
+
+    def takes(h, away):
+        each(half, lambda i: take(h * half + i, away))
+
+    for group in range(2):
+        give(region, 0, group, 0, True)
+        send(region, 0, group, n_in, True)
+    takes(0, 1)
+    takes(0, 2)
+    each(half, lambda i: spread(half + i))
+    takes(0, 3)
+    for group in range(2):
+        give(rest[0], 1, group, 0, False)
+        send(rest[0], 1, group, n_in, False)
+        if group == 0:
+            takes(1, 1)
+    takes(1, 2)
+    for group in range(2):
+        give_second(first_half, 0, group, ring, True)
+    takes(1, 3)
+    for group in range(2):
+        give(rest[1], 2, group, 0, False)
+        send(rest[1], 2, group, n_in, False)
     load_camera_out(col, 0)
     load_camera_out(mate, n_out)
     load_camera_out(across, 2 * n_out)
-    moments_sent(0, 0, every)
-    for h in range(2):
-        spread_done(h, halves[h])
-
-    def share(phase, k, c, away):
-        to_mate(phase, k, c).start()
-        if away:
-            to_across(phase, k, c).start()
+    for group in range(2):
+        give_second(second_half, 1, group, ring, False)
+    load_camera_in(col, ring)
+    spread_done()
 
     def finals(h):
         span = (h * half, half)
-        rest = (h * half, half, 1, rows - 1)
 
         def arrived(group, unit):
             @pl.when(h == 0)
@@ -735,7 +772,7 @@
                 y_copy(group, unit, 0, region).wait_recv()
 
             p_copy(group, unit, h, span).wait_recv()
-            y_copy(group, unit, 1 + h, rest).wait_recv()
+            y_copy(group, unit, 1 + h, (*span[:1], half, 1, rows - 1)).wait_recv()
 
         final_qkv(span, ring, (r.q_gain, r.k_gain), lambda which: arrived(0, which))
 
@@ -751,43 +788,36 @@
                 )
 
         each(rows, camera)
-
-        def ship(k):
-            def one(i):
-                c = h * half + i
-                to_mate(0, k, c).start()
-
-                @pl.when(h == 0)
-                def _():
-                    to_across(0, k, c).start()
-
-            each(half, one)
-
-        ship(0)
+        half_to_mate(0, h).start()
 
         def activate(unit):
             arrived(1, unit)
             raw = final(1, unit, span, ring + 3 + unit) + r.bias[col * ups + unit]
             value = (raw * (1.0 + lax.erf(raw * math.sqrt(0.5))) * 0.5).astype(BF16)
             r.hid1[own_place, unit, pl.ds(*span)] = shaped(value, (*span, 0, rows))
-            ship(unit + 1)
+            half_to_mate(unit + 1, h).start()
 
         each(ups, activate)
+
+        @pl.when(h == 0)
+        def _():
+            def ship(c):
+                to_across(0, 0, c).start()
+                each(ups, lambda unit: to_across(0, unit + 1, c).start())
+
+            each(half, ship)
 
         def fresh_out(slot, deep):
             @pl.when(h == 0)
             def _():
                 wait_out(slot, deep)
-
-        def arrived_mate(k):
-            each(half, lambda i: to_mate(0, k, h * half + i).wait_recv())
 
         def near_up(place):
             def one(unit):
                 slot = place * n_out + 1 + unit
                 fresh_out(slot, tile)
                 if place == mate_place:
-                    arrived_mate(unit + 1)
+                    half_to_mate(unit + 1, h).wait_recv()
                 add_tile(span, hid_value(place, unit + 1, span), slot)
 
             return one
@@ -796,7 +826,7 @@
         add_tile(span, hid_value(own_place, 0, span), 0, True)
         each(ups, near_up(own_place))
         fresh_out(n_out, wide)
-        arrived_mate(0)
+        half_to_mate(0, h).wait_recv()
         add_tile(span, hid_value(mate_place, 0, span), n_out)
         each(ups, near_up(mate_place))
 
@@ -807,14 +837,17 @@
     join_out_slots = (2 * n_out - 2, 2 * n_out - 1, ring + n_out, ring + n_out + 1)
     for place in range(4):
         load_out(r.w_join, join_out_slots[place], owners[place] * wide, wide)
+    for group in range(2):
+        all_sent(f_send[group], r.ys.at[group])
+        all_sent(p_send[group], r.ps.at[group])
 
     def far(c, k):
         ahead = k + AHEAD
-        later, kind = c + ahead // n_out, ahead % n_out
+        later = c + ahead // n_out
 
         @pl.when((later >= half) & (later < chunks))
         def _():
-            to_across(0, kind, later).start()
+            to_across(0, ahead % n_out, later).start()
 
         to_across(0, k, c).wait_recv()
         forward(0, k, c).start()
@@ -822,118 +855,131 @@
         @pl.when(c == 0)
         def _():
             wait_out(2 * n_out + k, wide if k == 0 else tile)
+
+        add_tile((c, 1), hid_value(across_place, k, (c, 1)), 2 * n_out + k)
+
+    def farther(c, k):
+        @pl.when(c == 0)
+        def _():
             wait_out(ring + k, wide if k == 0 else tile)
 
-        add_tile((c, 1), hid_value(across_place, k, (c, 1)), 2 * n_out + k)
         forward(0, k, c).wait_recv()
         add_tile((c, 1), hid_value(diag_place, k, (c, 1)), ring + k)
 
-    def norm_start(c):
-        sums_end(0, c)
-        total = accum[c, 0] + r.tokens[c].astype(F32) + r.down_bias[...].reshape(1, -1)
-        layer = total.astype(BF16)
-        r.layer[c] = layer
-        moments_start(1, 1 + c, pl.ds(c, 1), layer.astype(F32)[None])
-
-    def norm_end(c):
-        moments_end(1, 1 + c, pl.ds(c, 1), r.layer[pl.ds(c, 1)].astype(F32), r.join_gain)
-        spread(2 + c, (c, 1))
-
-    def steps(c):
+    def steps(c, pause=lambda k: None):
         def before(back, action):
+            if isinstance(c, int):
+                action(c - back)
+                return
+
             @pl.when(c >= back)
             def _():
                 action(c - back)
 
-        far(c, 0)
-        before(1, lambda b: sums(0, b, 1))
-        far(c, 1)
-        before(1, lambda b: sums(0, b, 2))
-        for k in range(2, n_out):
+        for k in range(n_out):
             far(c, k)
+            if k > 0:
+                farther(c, k - 1)
+            if k == 0:
+                before(3, norm_start)
+                before(4, norm_end)
+                before(5, relay)
+            if k == 1:
+                before(2, lambda b: sums(b, 2))
             if k == 2:
-                before(1, norm_start)
-        sums(0, c, 0)
-        before(1, norm_end)
-        for away in range(1, rows):
-            before(2, lambda b: take(2 + b, (b, 1), away))
-
-    each(chunks, steps)
+                before(1, lambda b: sums(b, 1))
+            pause(k)
+        farther(c, n_out - 1)
+        sums(c, 0)
+
+    queue = []
+    spans = ((0, 2), (2, 2), (4, 2), (6, 1), (7, 1))
+    second_spans = ((0, 4), (4, 2), (6, 1), (7, 1))
+    final_spans = (((0, 4), (0,), (0, 1)), ((4, 2), (1,), (2,)), ((6, 2), (2, 3), (3, 4)))
+
+    def whole(span):
+        return (*span, 0, rows)
+
+    def ready(i):
+        for c in range(spans[i][0], sum(spans[i])):
+            gathered(c)
+        give(whole(spans[i]), i, 0, 0, i == 0)
+        send(whole(spans[i]), i, 0, 3, i == 0, False)
+        for unit in range(3):
+            for c in range(spans[i][0], sum(spans[i])):
+                queue.append((unit, i, whole((c, 1))))
+
+    def issue(count):
+        for _ in range(count):
+            if queue:
+                unit, i, part = queue.pop(0)
+                y_copy(0, unit, i, part).start()
+
+    def join_second(i):
+        give_second(second_spans[i], i, 0, 2 * n_out, i == 0)
+
+    def join_final(i):
+        span, p_stages, y_stages = final_spans[i]
+
+        def arrived(which):
+            if i == 0:
+                wait_in(ring + which, wide)
+            for stage in p_stages:
+                p_copy(0, which, stage, second_spans[stage]).wait_recv()
+            for stage in y_stages:
+                y_copy(0, which, stage, whole(spans[stage])).wait_recv()
+
+        final_qkv(span, ring, (r.jq_gain, r.jk_gain), arrived)
+
+    each(last, steps)
+    ready(0)
+    steps(last, lambda k: issue(1 if k else 0))
     load_join_in(mate, 2 * n_out)
     load_join_in(col, ring)
-
-    def shared(c):
-        for k in range(n_out):
-            to_across(0, k, c).wait_send()
-            to_mate(0, k, c).wait_send()
-            forward(0, k, c).wait_send()
-
-    each(chunks, shared)
-    for group in range(2):
-
-        def sent(unit):
-            y_copy(group, unit, 0, region).wait_send()
-            for h in range(2):
-                y_copy(group, unit, 1 + h, (h * half, half, 1, rows - 1)).wait_send()
-                p_copy(group, unit, h, (h * half, half)).wait_send()
-
-        each(counts[group], sent)
-
-    spans = [(last - 1, 1), (last, 1)]
-    if chunks > 2:
-        spans.insert(0, (0, last - 1))
-    regions = [(*span, 0, rows) for span in spans]
-    n_spans = len(spans)
-
-    def join_give(i, fresh=False):
-        give(regions[i], 3 + i, (0,), 0, fresh)
-
-    def join_send(i, fresh=False):
-        send(regions[i], 3 + i, (0,), 3, fresh)
-
-    def join_second(i, fresh=False):
-        give_second(spans[i], 2 + i, (0,), 2 * n_out, fresh)
-
-    def join_final(i, fresh=False):
-        def arrived(which):
-            if fresh:
-                wait_in(ring + which, wide)
-            p_copy(0, which, 2 + i, spans[i]).wait_recv()
-            y_copy(0, which, 3 + i, regions[i]).wait_recv()
-
-        final_qkv(spans[i], ring, (r.jq_gain, r.jk_gain), arrived)
-
-    def take_one(c, away):
-        take(2 + c, (c, 1), away)
-
-    main = n_spans == 3
-    if main:
-        join_give(0, True)
-    sums(0, last, 1)
-    take_one(last - 1, 1)
-    if main:
-        join_send(0, True)
-    sums(0, last, 2)
-    take_one(last - 1, 2)
-    if main:
-        join_second(0, True)
-    norm_start(last)
-    take_one(last - 1, 3)
-    join_give(n_spans - 2, not main)
-    join_send(n_spans - 2, not main)
-    norm_end(last)
-    join_second(n_spans - 2, not main)
-    if main:
-        join_final(0, True)
-    take_one(last, 1)
-    take_one(last, 2)
-    join_final(n_spans - 2, not main)
-    take_one(last, 3)
-    join_give(n_spans - 1)
-    join_send(n_spans - 1)
-    join_second(n_spans - 1)
-    sums_sent(0)
-    join_final(n_spans - 1)
+    norm_end(4)
+    norm_start(5)
+    issue(1)
+    relay(3)
+    sums(6, 2)
+    issue(1)
+    sums(7, 1)
+    norm_end(5)
+    issue(1)
+    relay(4)
+    norm_start(6)
+    ready(1)
+    issue(1)
+    sums(7, 2)
+    issue(1)
+    relay(5)
+    norm_end(6)
+    issue(1)
+    join_second(0)
+    issue(1)
+    norm_start(7)
+    issue(2)
+    ready(2)
+    relay(6)
+    norm_end(7)
+    issue(2)
+    join_final(0)
+    issue(2)
+    join_second(1)
+    issue(2)
+    ready(3)
+    issue(len(queue))
+    relay(7)
+    join_second(2)
+    all_sent(r.z_send, r.z_sent.at[0])
+    for which, buffer in enumerate((r.hid0, r.hid1)):
+        all_sent(buffer.at[own_place], r.a_send.at[which])
+        all_sent(buffer.at[own_place], r.b_send.at[which])
+        all_sent(buffer.at[own_place], r.d_send.at[which])
+    ready(4)
+    issue(len(queue))
+    join_second(3)
+    join_final(1)
+    join_final(2)
 
     def blend(c):
         for start in range(0, wide, HEAD_DIM):
@@ -945,71 +991,79 @@
             )
             r.hid0[own_place, c, :, :, head] = soft_blend(q, k, v).reshape(rows, piece, HEAD_DIM)
         to_across(1, 0, c).start()
-        to_mate(1, 0, c).start()
+        to_mate(c).start()
+
+    def hand_on(c):
+        to_across(1, 0, c).wait_recv()
+        forward(1, 0, c).start()
 
     def result_of(c):
-        sums_end(1, c)
+        sums_end(c)
         r.result[c] = (accum[c, 0] + r.layer[c].astype(F32)).astype(BF16)
 
-    lead = min(2, chunks)
-    each(lead, blend)
+    blend(0)
+    blend(1)
     for slot in join_out_slots:
         wait_out(slot, wide)
+    hand_on(0)
 
     def join_steps(c):
-        def add(place, begin=False):
-            add_tile((c, 1), hid_value(place, 0, (c, 1)), join_out_slots[place], begin)
-
-        @pl.when(c + lead < chunks)
-        def _():
-            blend(c + lead)
+        def before(back, action):
+            @pl.when(c >= back)
+            def _():
+                action(c - back)
+
+        def add(place, start=False):
+            add_tile((c, 1), hid_value(place, 0, (c, 1)), join_out_slots[place], start)
 
         add(own_place, True)
-        to_mate(1, 0, c).wait_recv()
+        to_mate(c).wait_recv()
         add(mate_place)
-        to_across(1, 0, c).wait_recv()
-        forward(1, 0, c).start()
         add(across_place)
         forward(1, 0, c).wait_recv()
         add(diag_place)
-        sums(1, c, 0)
-
-        @pl.when(c >= 1)
+        sums(c, 0)
+
+        @pl.when(c + 2 < chunks)
         def _():
-            sums(1, c - 1, 1)
-            sums(1, c - 1, 2)
-
-        @pl.when(c >= 2)
+            blend(c + 2)
+
+        before(1, lambda b: sums(b, 1))
+
+        @pl.when(c + 1 < chunks)
         def _():
-            result_of(c - 2)
+            hand_on(c + 1)
+
+        before(2, lambda b: sums(b, 2))
+        before(3, result_of)
 
     each(chunks, join_steps)
-    sums(1, last, 1)
-    sums(1, last, 2)
+    sums(last - 1, 2)
+    sums(last, 1)
+    result_of(last - 2)
+    sums(last, 2)
     result_of(last - 1)
     result_of(last)
 
-    sums_sent(1)
-
-    def drained(c):
-        to_across(1, 0, c).wait_send()
-        to_mate(1, 0, c).wait_send()
-        forward(1, 0, c).wait_send()
-        moments_sent(1, 1 + c, pl.ds(c, 1))
-        spread_done(2 + c, (c, 1))
-
-    each(chunks, drained)
-    for i in range(n_spans):
-
-        def sent_join(unit):
-            y_copy(0, unit, 3 + i, regions[i]).wait_send()
-            p_copy(0, unit, 2 + i, spans[i]).wait_send()
-
-        each(3, sent_join)
-
-
-AHEAD = 3
-CHUNKS = 4
+    all_sent(r.z_send, r.z_sent.at[0])
+    all_sent(r.hid0.at[own_place], r.a_send.at[0])
+    all_sent(r.hid0.at[own_place], r.b_send.at[0])
+    all_sent(r.hid0.at[own_place], r.d_send.at[0])
+    all_sent(f_send[0], r.ys.at[0])
+    all_sent(p_send[0], r.ps.at[0])
+    inner = (row > 0) & (row < rows - 1)
+
+    @pl.when(inner)
+    def _():
+        all_sent(normed, r.g_send.at[2])
+
+    @pl.when(jnp.logical_not(inner))
+    def _():
+        all_sent(normed.at[:, pl.ds(0, 2)], r.g_send.at[2])
+
+
+AHEAD = 5
+CHUNKS = 8
 
 
 def tile_of(depth, columns, cols):
@@ -1076,32 +1130,37 @@
     dma, vmem = pltpu.SemaphoreType.DMA, pltpu.VMEM
     scratch = {
         "pool": vmem((3 * n_in * slot_pieces, tile, tile), BF16),
-        "pool_sem": dma((3 * n_in * slot_pieces,)),
+        "pool_sem": dma((3 * n_in,)),
         "normed": vmem((chunks, rows, piece, depth), BF16),
-        "moments": vmem((2, 4, chunks, piece, HEAD_DIM), F32),
-        "m_send": dma((1 + chunks, 3)),
-        "m_recv": dma((1 + chunks, 3)),
-        "g_right": dma((2 + chunks, rows)),
-        "g_left": dma((2 + chunks, rows)),
-        "g_arrive": dma((2 + chunks, rows)),
+        "start": vmem((4, 16, HEAD_DIM), F32),
+        "moments": vmem((4, chunks, piece, HEAD_DIM), F32),
+        "m_send": dma((chunks // 2 + 1, 3)),
+        "m_recv": dma((chunks // 2 + 1, 3)),
+        "g_send": dma((3,)),
+        "g_arrive": dma((chunks, rows)),
         "qkv": vmem((3, chunks, rows, piece, wide), BF16),
         "hid0": vmem((4, chunks, rows, piece, wide), BF16),
         "hid1": vmem((4, ups, chunks, rows, piece, tile), BF16),
         "accum": vmem((chunks, rows, piece, width), F32),
-        "z_send": vmem((chunks, rows, piece, width), BF16),
-        "z_left": vmem((chunks, rows, piece, width), BF16),
-        "z_right": vmem((chunks, rows, piece, width), BF16),
+        "z_send": vmem((chunks, rows - 1, piece, width), BF16),
+        "z_in": vmem((chunks, rows + 1, piece, width), BF16),
+        "z_sent": dma((1,)),
+        "z_arrive": dma((chunks, rows + 1)),
         "layer": vmem((chunks, piece, width), BF16),
+        "a_recv": dma((n_out, chunks)),
+        "b_recv": dma((n_out, 2)),
+        "d_recv": dma((n_out, 2)),
+        "ys": dma((2,)),
+        "ps": dma((2,)),
     }
-    for name in ("zr_send", "zr_recv", "zl_send", "zl_recv"):
-        scratch[name] = dma((2, chunks, rows))
-    for name in ("a_send", "a_recv", "b_send", "b_recv", "d_send", "d_recv"):
-        scratch[name] = dma((n_out + 1, chunks))
+    for name in ("a_send", "b_send", "d_send"):
+        scratch[name] = dma((2,))
     for group, (count, wid) in enumerate(((3, wide), (ups, tile))):
         for name in ("f_send", "f_recv", "y_recv", "p_send", "p_recv"):
             scratch[name + str(group)] = vmem((count, chunks, rows, piece, wid), BF16)
-        for name in ("fs", "fr", "ys", "yr", "ps", "pr"):
-            scratch[name + str(group)] = dma((count, 6))
+        scratch["fs" + str(group)] = dma((count,))
+        for name in ("fr", "yr", "pr"):
+            scratch[name + str(group)] = dma((count, 3 if group else 5))
     names = (*inputs, "result", *scratch)
     joined = pl.pallas_call(
         functools.partial(layer_kernel, names, float(depth * cols)),
@@ -1129,6 +1188,7 @@
     wide = arrays[2].shape[1] // lax.axis_size("cols")
     good = (
         own_rows == 2 * TOK_CAM
+        and own_rows == HEAD_DIM
         and tile * ups * lax.axis_size("cols") == up_weight.shape[1]
         and tile % HEAD_DIM == 0
         and depth % tile == 0

time: 240 us -> 196 us (0.82)
  Pallas kernels: 238 us -> 194 us
    pallas_call x1, Pallas kernels: 238 us -> 194 us  [kernel_body(): pl.pallas_call(functools.partial(layer_kernel, names, float(depth * cols)...]
where the time goes in v2:
time: 196 us
  Pallas kernels  194 us (99%)
    pallas_call x1, Pallas kernels, kernel_body(): pl.pallas_call(functools.partial(layer_kernel, names, float(depth * cols)...  194 us

profile of v2, /device:TPU:0, one launch (start us, length us, event | category | flops | bytes accessed | tf_op | source)
XLA Modules:
  0.0 195.8 jit_solution(9072821393422279665)
XLA Ops:
  0.0 194.1 %layer.1 = bf16[8,16,1536]{2,1,0:T(8,128)(2,1)} custom-call(bf16[8,16,1536]{2,1,0:T(8,128)(2,1)} %bitcast.18, f32[1536]{0:T(1024)} %refs_1_.1, f32[1536]{0:T(1024)} %refs_2_.1, f32[1536]{0:T(1024)} %refs_3_.1, f32[12,1,512]{2,1,0:T(1,128)} %bitcast.19, f32[1536]{0:T(1024)} %refs_5_.1, f32[1536]{0:T(1024)} %refs_6_.1, f32[1536]{0:T(1024)} %refs_7_.1, ...), custom_call_target="tpu_custom_call" | custom-call | tf_op jit(solution)/shard_map/layer/pallas_call | solution.py:1165
  194.1 1.8 copy.21

commit v3 on v2

--- a/solution.py
+++ b/solution.py
@@ -564,60 +564,37 @@
             {"cols": mate},
         )
 
-    def z_right(c, rel):
-        return remote(
-            r.z_send.at[c, rel - 1],
-            r.z_in.at[c, rel - 1],
-            r.z_sent.at[0],
-            r.z_arrive.at[c, rel - 1],
-            {"rows": row + 1},
-        )
-
-    def z_left(c, rel):
-        there = (rel + 1) % rows or rows
-        return remote(
-            r.z_send.at[c, rel - 1],
-            r.z_in.at[c, there],
-            r.z_sent.at[0],
-            r.z_arrive.at[c, there],
-            {"rows": row - 1},
-        )
-
     def z_wait(c, place):
         part = r.z_in.at[c, place]
         pltpu.make_async_copy(part, part, r.z_arrive.at[c, place]).wait()
 
     def sums(c, step):
-        def go(rel, move):
-            value = accum[c, rel]
-            if step > 0:
-                z_wait(c, rel)
-                value += r.z_in[c, rel].astype(F32)
-            r.z_send[c, rel - 1] = value.astype(BF16)
-            move(c, rel).start()
-
-        @pl.when(row == step)
-        def _():
-            for block in range(rows - 1, step, -1):
-                go(block - step, z_right)
-
-        here = rows - 1 - step
-
-        @pl.when(row == here)
-        def _():
-            for block in range(here):
-                go(block - here + rows, z_left)
+        for place, moves in enumerate(SUM_MOVES[step]):
+
+            @pl.when(row == place)
+            def _():
+                for block, there in moves:
+                    rel = (block - place) % rows
+                    value = accum[c, rel]
+                    if step > 0:
+                        z_wait(c, rel)
+                        value += r.z_in[c, rel].astype(F32)
+                    r.z_send[c, rel - 1] = value.astype(BF16)
+                    slot = (block - there) % rows
+                    if step == 0 and slot == 0:
+                        slot = rows
+                    remote(
+                        r.z_send.at[c, rel - 1],
+                        r.z_in.at[c, slot],
+                        r.z_sent.at[0],
+                        r.z_arrive.at[c, slot],
+                        {"rows": there},
+                    ).start()
 
     def sums_end(c):
-        @pl.when(row > 0)
-        def _():
-            z_wait(c, 0)
-            accum[c, 0] += r.z_in[c, 0].astype(F32)
-
-        @pl.when(row < rows - 1)
-        def _():
-            z_wait(c, rows)
-            accum[c, 0] += r.z_in[c, rows].astype(F32)
+        z_wait(c, rows)
+        z_wait(c, 0)
+        accum[c, 0] += r.z_in[c, rows].astype(F32) + r.z_in[c, 0].astype(F32)
 
     others = (mate, across, diagonal)
 
@@ -703,11 +680,11 @@
     load_camera_in(diagonal, 0)
     load_camera_in(across, n_in)
     load_camera_in(mate, ring)
-    greet(3)
     own = r.tokens[...].reshape(chunks * piece, depth).astype(F32)
     few = r.start.shape[1]
     begin = HEAD_DIM // 2 - few // 2
     r.start[3] = jnp.transpose(pairs(own))[begin : begin + few]
+    greet(3)
     swaps = [
         remote(
             r.start.at[3],
@@ -880,12 +857,12 @@
             far(c, k)
             if k > 0:
                 farther(c, k - 1)
-            if k == 0:
-                before(3, norm_start)
-                before(4, norm_end)
-                before(5, relay)
             if k == 1:
-                before(2, lambda b: sums(b, 2))
+                before(2, norm_start)
+            if k == 1:
+                before(3, norm_end)
+            if k == 1:
+                before(4, relay)
             if k == 2:
                 before(1, lambda b: sums(b, 1))
             pause(k)
@@ -894,8 +871,8 @@
 
     queue = []
     spans = ((0, 2), (2, 2), (4, 2), (6, 1), (7, 1))
-    second_spans = ((0, 4), (4, 2), (6, 1), (7, 1))
-    final_spans = (((0, 4), (0,), (0, 1)), ((4, 2), (1,), (2,)), ((6, 2), (2, 3), (3, 4)))
+    second_spans = ((0, 4), (4, 2), (6, 2))
+    final_spans = (((0, 4), (0,), (0, 1)), ((4, 2), (1,), (2,)), ((6, 2), (2,), (3, 4)))
 
     def whole(span):
         return (*span, 0, rows)
@@ -936,40 +913,28 @@
     steps(last, lambda k: issue(1 if k else 0))
     load_join_in(mate, 2 * n_out)
     load_join_in(col, ring)
-    norm_end(4)
-    norm_start(5)
     issue(1)
-    relay(3)
-    sums(6, 2)
+    norm_end(5)
+    sums(7, 1)
+    norm_start(6)
+    issue(2)
+    relay(4)
+    relay(5)
+    ready(1)
+    norm_end(6)
+    norm_start(7)
+    issue(3)
+    join_second(0)
+    relay(6)
     issue(1)
-    sums(7, 1)
-    norm_end(5)
-    issue(1)
-    relay(4)
-    norm_start(6)
-    ready(1)
-    issue(1)
-    sums(7, 2)
-    issue(1)
-    relay(5)
-    norm_end(6)
-    issue(1)
-    join_second(0)
-    issue(1)
-    norm_start(7)
+    norm_end(7)
     issue(2)
     ready(2)
-    relay(6)
-    norm_end(7)
-    issue(2)
-    join_final(0)
-    issue(2)
+    issue(4)
     join_second(1)
-    issue(2)
+    relay(7)
     ready(3)
     issue(len(queue))
-    relay(7)
-    join_second(2)
     all_sent(r.z_send, r.z_sent.at[0])
     for which, buffer in enumerate((r.hid0, r.hid1)):
         all_sent(buffer.at[own_place], r.a_send.at[which])
@@ -977,7 +942,8 @@
         all_sent(buffer.at[own_place], r.d_send.at[which])
     ready(4)
     issue(len(queue))
-    join_second(3)
+    join_second(2)
+    join_final(0)
     join_final(1)
     join_final(2)
 
@@ -1005,7 +971,6 @@
     blend(1)
     for slot in join_out_slots:
         wait_out(slot, wide)
-    hand_on(0)
 
     def join_steps(c):
         def before(back, action):
@@ -1019,6 +984,11 @@
         add(own_place, True)
         to_mate(c).wait_recv()
         add(mate_place)
+
+        @pl.when(c == 0)
+        def _():
+            hand_on(c)
+
         add(across_place)
         forward(1, 0, c).wait_recv()
         add(diag_place)
@@ -1034,14 +1004,11 @@
         def _():
             hand_on(c + 1)
 
-        before(2, lambda b: sums(b, 2))
         before(3, result_of)
 
     each(chunks, join_steps)
-    sums(last - 1, 2)
     sums(last, 1)
     result_of(last - 2)
-    sums(last, 2)
     result_of(last - 1)
     result_of(last)
 
@@ -1062,7 +1029,11 @@
         all_sent(normed.at[:, pl.ds(0, 2)], r.g_send.at[2])
 
 
-AHEAD = 5
+AHEAD = 4
+SUM_MOVES = (
+    (((3, 1), (2, 1), (1, 1)), ((0, 0),), ((3, 3),), ((0, 2), (1, 2), (2, 2))),
+    ((), ((3, 3), (2, 2)), ((0, 0), (1, 1)), ()),
+)
 CHUNKS = 8
 
 

time: 196 us -> 191 us (0.974)
  Pallas kernels: 194 us -> 189 us
    pallas_call x1, Pallas kernels: 194 us -> 189 us  [kernel_body(): pl.pallas_call(functools.partial(layer_kernel, names, float(depth * cols)...]
where the time goes in v3:
time: 191 us; the launch traced here: 190 us
  Pallas kernels  189 us (99%)
    pallas_call x1, Pallas kernels, kernel_body(): pl.pallas_call(functools.partial(layer_kernel, names, float(depth * cols)...  189 us

profile of v3, /device:TPU:0, one launch (start us, length us, event | category | flops | bytes accessed | tf_op | source)
XLA Modules:
  0.0 190.4 jit_solution(17694824121967681580)
XLA Ops:
  0.0 188.6 %layer.1 = bf16[8,16,1536]{2,1,0:T(8,128)(2,1)} custom-call(bf16[8,16,1536]{2,1,0:T(8,128)(2,1)} %bitcast.18, f32[1536]{0:T(1024)} %refs_1_.1, f32[1536]{0:T(1024)} %refs_2_.1, f32[1536]{0:T(1024)} %refs_3_.1, f32[12,1,512]{2,1,0:T(1,128)} %bitcast.19, f32[1536]{0:T(1024)} %refs_5_.1, f32[1536]{0:T(1024)} %refs_6_.1, f32[1536]{0:T(1024)} %refs_7_.1, ...), custom_call_target="tpu_custom_call" | custom-call | tf_op jit(solution)/shard_map/layer/pallas_call | solution.py:1136
  188.6 1.8 copy.21

commit v4 on v3

--- a/solution.py
+++ b/solution.py
@@ -915,12 +915,14 @@
     load_join_in(col, ring)
     issue(1)
     norm_end(5)
+    issue(1)
+    ready(1)
     sums(7, 1)
+    issue(2)
     norm_start(6)
     issue(2)
     relay(4)
     relay(5)
-    ready(1)
     norm_end(6)
     norm_start(7)
     issue(3)

time: 191 us -> 193 us (1.010)
  Pallas kernels: 189 us -> 191 us
    pallas_call x1, Pallas kernels: 189 us -> 191 us  [kernel_body(): pl.pallas_call(functools.partial(layer_kernel, names, float(depth * cols)...]
where the time goes in v4:
time: 193 us
  Pallas kernels  191 us (99%)
    pallas_call x1, Pallas kernels, kernel_body(): pl.pallas_call(functools.partial(layer_kernel, names, float(depth * cols)...  191 us

profile of v4, /device:TPU:0, one launch (start us, length us, event | category | flops | bytes accessed | tf_op | source)
XLA Modules:
  0.0 192.7 jit_solution(11872652934238844554)
XLA Ops:
  0.0 191.0 %layer.1 = bf16[8,16,1536]{2,1,0:T(8,128)(2,1)} custom-call(bf16[8,16,1536]{2,1,0:T(8,128)(2,1)} %bitcast.18, f32[1536]{0:T(1024)} %refs_1_.1, f32[1536]{0:T(1024)} %refs_2_.1, f32[1536]{0:T(1024)} %refs_3_.1, f32[12,1,512]{2,1,0:T(1,128)} %bitcast.19, f32[1536]{0:T(1024)} %refs_5_.1, f32[1536]{0:T(1024)} %refs_6_.1, f32[1536]{0:T(1024)} %refs_7_.1, ...), custom_call_target="tpu_custom_call" | custom-call | tf_op jit(solution)/shard_map/layer/pallas_call | solution.py:1138
  191.0 1.8 copy.21

commit v5 on v3

--- a/solution.py
+++ b/solution.py
@@ -919,8 +919,8 @@
     norm_start(6)
     issue(2)
     relay(4)
+    ready(1)
     relay(5)
-    ready(1)
     norm_end(6)
     norm_start(7)
     issue(3)

time: 191 us -> 189 us (0.990)
  Pallas kernels: 189 us -> 187 us
where the time goes in v5:
time: 189 us
  Pallas kernels  187 us (99%)
    pallas_call x1, Pallas kernels, kernel_body(): pl.pallas_call(functools.partial(layer_kernel, names, float(depth * cols)...  187 us

profile of v5, /device:TPU:0, one launch (start us, length us, event | category | flops | bytes accessed | tf_op | source)
XLA Modules:
  0.0 189.1 jit_solution(10909383079867668976)
XLA Ops:
  0.0 187.3 %layer.1 = bf16[8,16,1536]{2,1,0:T(8,128)(2,1)} custom-call(bf16[8,16,1536]{2,1,0:T(8,128)(2,1)} %bitcast.18, f32[1536]{0:T(1024)} %refs_1_.1, f32[1536]{0:T(1024)} %refs_2_.1, f32[1536]{0:T(1024)} %refs_3_.1, f32[12,1,512]{2,1,0:T(1,128)} %bitcast.19, f32[1536]{0:T(1024)} %refs_5_.1, f32[1536]{0:T(1024)} %refs_6_.1, f32[1536]{0:T(1024)} %refs_7_.1, ...), custom_call_target="tpu_custom_call" | custom-call | tf_op jit(solution)/shard_map/layer/pallas_call | solution.py:1136
  187.3 1.8 copy.21
